TPU v7x, 32 devices: a 4x4x1 block of a 4x4x8 slice. The times are simulated.
32 devices in a mesh: dp: 1 (over z), sw: 4 (over y), sh: 8 (over x, core).
Axes of the slice: x: 4, y: 4, z: 1, core: 2. Of those that a mesh axis runs over, the one named last changes fastest.
The devices are a block of a 4x4x8 slice.
Arguments:
- features: bfloat16 [1, 512, 6, 96, 24], P('dp', None, None, 'sh', 'sw')
- latent: bfloat16 [1, 16, 6, 96, 24], P('dp', None, None, 'sh', 'sw')
- gn_gain: float32 [2, 2, 512], replicated
- gn_bias: float32 [2, 2, 512], replicated
- zy_weight: bfloat16 [2, 2, 16, 512], replicated
- zy_bias: float32 [2, 2, 512], replicated
- zb_weight: bfloat16 [2, 2, 16, 512], replicated
- zb_bias: float32 [2, 2, 512], replicated
- conv_weight: bfloat16 [2, 2, 512, 512, 3, 3, 3], replicated
- conv_bias: float32 [2, 2, 512], replicated
- up_weight: bfloat16 [512, 512, 3, 3], replicated
- up_bias: float32 [512], replicated
Outputs:
- output: bfloat16 [1, 512, 6, 192, 48], P('dp', None, None, 'sh', 'sw')
All inputs are finite; a program needn't handle non-finite values.
Results may differ from a plain program's by a relative error of at most 0.0137178.
Values are sent between devices in bfloat16 or wider.
A program may use at most 768 MiB of HBM per device.

v0:
```python
import jax
import jax.numpy as jnp
from jax import lax
from jax.sharding import PartitionSpec as P

NUM_GROUPS = 32
GN_EPSILON = 1e-6
CONV_DIMS = ("NCDHW", "OIDHW", "NCDHW")


def solution(mesh):
    n_sh = mesh.shape["sh"]
    n_sw = mesh.shape["sw"]

    def per_channel(values):
        return values[None, :, None, None, None]

    def edge_exchange(values, axis_name, n_dev, dim):
        n_len = values.shape[dim]
        tail = lax.slice_in_dim(values, n_len - 1, n_len, axis=dim)
        head = lax.slice_in_dim(values, 0, 1, axis=dim)
        if n_dev == 1:
            from_prev = jnp.zeros_like(tail)
            from_next = jnp.zeros_like(head)
        else:
            from_prev = lax.ppermute(tail, axis_name, [(i, i + 1) for i in range(n_dev - 1)])
            from_next = lax.ppermute(head, axis_name, [(i + 1, i) for i in range(n_dev - 1)])
        return jnp.concatenate([from_prev, values, from_next], axis=dim)

    def with_border(values):
        return edge_exchange(edge_exchange(values, "sh", n_sh, 3), "sw", n_sw, 4)

    def group_norm(values, gain, shift):
        n_batch, n_chan, n_frame, n_row, n_col = values.shape
        grouped = values.astype(jnp.float32).reshape(n_batch, NUM_GROUPS, n_chan // NUM_GROUPS, n_frame, n_row, n_col)
        local_stats = jnp.stack([jnp.sum(grouped, axis=(2, 3, 4, 5)), jnp.sum(jnp.square(grouped), axis=(2, 3, 4, 5))])
        total_stats = lax.psum(local_stats, ("sh", "sw"))
        count = (n_chan // NUM_GROUPS) * n_frame * n_row * n_col * n_sh * n_sw
        group_mean = total_stats[0] / count
        group_var = jnp.maximum(total_stats[1] / count - jnp.square(group_mean), 0.0)
        inv_std = lax.rsqrt(group_var + GN_EPSILON)
        normed = (grouped - group_mean[:, :, None, None, None, None]) * inv_std[:, :, None, None, None, None]
        return normed.reshape(values.shape) * per_channel(gain) + per_channel(shift)

    def latent_map(latent, weight, bias):
        return jnp.einsum("nzthw,zc->ncthw", latent, weight, preferred_element_type=jnp.float32) + per_channel(bias)

    def causal_conv(bordered, weight, bias):
        first_frame = bordered[:, :, :1]
        padded = jnp.concatenate([first_frame, first_frame, bordered], axis=2)
        conv_out = lax.conv_general_dilated(padded, weight, (1, 1, 1), "VALID", dimension_numbers=CONV_DIMS, preferred_element_type=jnp.float32)
        return (conv_out + per_channel(bias)).astype(jnp.bfloat16)

    def upsample_conv(bordered, weight, bias):
        upsampled = jnp.repeat(jnp.repeat(bordered, 2, axis=3), 2, axis=4)
        n_row = upsampled.shape[3]
        n_col = upsampled.shape[4]
        cropped = upsampled[:, :, :, 1:n_row - 1, 1:n_col - 1]
        conv_out = lax.conv_general_dilated(cropped, weight[:, :, None], (1, 1, 1), "VALID", dimension_numbers=CONV_DIMS, preferred_element_type=jnp.float32)
        return (conv_out + per_channel(bias)).astype(jnp.bfloat16)

    def local_step(features, latent, gn_gain, gn_bias, zy_weight, zy_bias, zb_weight, zb_bias, conv_weight, conv_bias, up_weight, up_bias):
        hidden = features
        for block in range(gn_gain.shape[0]):
            branch = hidden
            for slot in range(2):
                normed = group_norm(branch, gn_gain[block, slot], gn_bias[block, slot])
                mixed = normed * latent_map(latent, zy_weight[block, slot], zy_bias[block, slot]) + latent_map(latent, zb_weight[block, slot], zb_bias[block, slot])
                activated = jax.nn.silu(mixed).astype(jnp.bfloat16)
                branch = causal_conv(with_border(activated), conv_weight[block, slot], conv_bias[block, slot])
            hidden = (hidden.astype(jnp.float32) + branch.astype(jnp.float32)).astype(jnp.bfloat16)
        return upsample_conv(with_border(hidden), up_weight, up_bias)

    data_spec = P("dp", None, None, "sh", "sw")
    return jax.shard_map(local_step, mesh=mesh, in_specs=(data_spec, data_spec) + (P(),) * 10, out_specs=data_spec, check_vma=False)
```

profile of v0, /device:TPU:97, one launch (start us, length us, event | category | flops | bytes accessed | tf_op | source)
XLA Modules:
  0.0 496.4 jit_solution(7131802384957554061)
XLA Ops:
  0.0 1.4 convert_reduce_fusion.1
  1.8 49.8 %psum.28 = f32[2,1,32]{2,1,0:T(1,128)S(1)} all-reduce(f32[2,1,32]{2,1,0:T(1,128)S(1)} %pad_maximum_fusion.31), channel_id=1, replica_groups=mesh['dp'=1,'sw'=4,'sh'=8] {'sh','sw'}, use_global_device_ids=true, to_apply=%region_4.5 | all-reduce | flops 64 | bytes 512 | tf_op jit(solution)/shard_map/psum | solution.py:37
  51.6 1.4 fusion.101
  53.0 1.4 fusion.102
  54.3 1.4 fusion.103
  55.7 1.4 fusion.100
  57.4 1.6 fusion.26
  59.0 0.5 fusion.56
  59.6 2.0 collective-permute-start
  61.6 2.4 collective-permute-start.1
  64.0 3.2 collective-permute-done.1
  67.4 2.4 collective-permute-start.2
  69.8 1.3 collective-permute-start.3
  71.2 0.6 fusion.99
  71.8 3.5 collective-permute-done.3
  75.3 0.5 maximum_maximum_fusion
  75.8 35.5 %fusion.6 = f32[1,512,6,12,6]{1,0,4,3,2:T(1,128)S(1)} fusion(bf16[2,2,512,512,3,3,3]{3,2,6,5,4,1,0:T(8,128)(2,1)} %param.20, bf16[1,512,8,14,8]{1,3,4,2,0:T(8,128)(2,1)S(1)} %maximum_maximum_fusion), kind=kOutput, calls=%fused_computation.6 | convolution fusion | flops 6115295232 | bytes 15958016 | tf_op jit(solution)/shard_map/conv_general_dilated | solution.py:51
  111.9 45.1 %psum.29 = f32[2,1,32]{2,1,0:T(1,128)S(1)} all-reduce(f32[2,1,32]{2,1,0:T(1,128)S(1)} %pad_maximum_fusion.32), channel_id=1, replica_groups=mesh['dp'=1,'sw'=4,'sh'=8] {'sh','sw'}, use_global_device_ids=true, to_apply=%region_9.10 | all-reduce | flops 64 | bytes 512 | tf_op jit(solution)/shard_map/psum | solution.py:37
  157.4 0.5 fusion.24
  157.9 0.5 fusion.55
  158.5 2.1 collective-permute-start.4
  160.7 2.3 collective-permute-start.5
  162.9 3.4 collective-permute-done.5
  166.5 2.3 collective-permute-start.6
  168.7 1.3 collective-permute-start.7
  170.4 3.8 collective-permute-done.7
  174.2 0.5 maximum_maximum_fusion.1
  174.7 35.1 %fusion.4 = f32[1,512,6,12,6]{1,0,4,3,2:T(1,128)S(1)} fusion(bf16[2,2,512,512,3,3,3]{3,2,6,5,4,1,0:T(8,128)(2,1)} %param.20, bf16[1,512,8,14,8]{1,3,4,2,0:T(8,128)(2,1)S(1)} %maximum_maximum_fusion.1), kind=kOutput, calls=%fused_computation.4 | convolution fusion | flops 6115295232 | bytes 15958016 | tf_op jit(solution)/shard_map/conv_general_dilated | solution.py:51
  209.9 0.4 convert_reduce_fusion
  210.7 45.0 %psum.30 = f32[2,1,32]{2,1,0:T(1,128)S(1)} all-reduce(f32[2,1,32]{2,1,0:T(1,128)S(1)} %pad_maximum_fusion.33), channel_id=1, replica_groups=mesh['dp'=1,'sw'=4,'sh'=8] {'sh','sw'}, use_global_device_ids=true, to_apply=%region_14.15 | all-reduce | flops 64 | bytes 512 | tf_op jit(solution)/shard_map/psum | solution.py:37
  256.0 0.4 fusion.22
  256.5 0.5 fusion.54
  257.2 2.1 collective-permute-start.8
  259.3 2.3 collective-permute-start.9
  261.6 3.4 collective-permute-done.9
  265.1 2.3 collective-permute-start.10
  267.4 1.3 collective-permute-start.11
  269.0 3.8 collective-permute-done.11
  272.8 0.5 maximum_maximum_fusion.2
  273.3 35.5 %fusion.2 = f32[1,512,6,12,6]{1,0,4,3,2:T(1,128)S(1)} fusion(bf16[2,2,512,512,3,3,3]{3,2,6,5,4,1,0:T(8,128)(2,1)} %param.20, bf16[1,512,8,14,8]{1,3,4,2,0:T(8,128)(2,1)S(1)} %maximum_maximum_fusion.2), kind=kOutput, calls=%fused_computation.2 | convolution fusion | flops 6115295232 | bytes 15958016 | tf_op jit(solution)/shard_map/conv_general_dilated | solution.py:51
  309.5 45.1 %psum.31 = f32[2,1,32]{2,1,0:T(1,128)S(1)} all-reduce(f32[2,1,32]{2,1,0:T(1,128)S(1)} %pad_maximum_fusion.34), channel_id=1, replica_groups=mesh['dp'=1,'sw'=4,'sh'=8] {'sh','sw'}, use_global_device_ids=true, to_apply=%region_19.20 | all-reduce | flops 64 | bytes 512 | tf_op jit(solution)/shard_map/psum | solution.py:37
  354.9 0.5 fusion.20
  355.6 0.5 fusion.53
  356.2 2.1 collective-permute-start.12
  358.4 2.3 collective-permute-start.13
  360.6 3.4 collective-permute-done.13
  364.2 2.2 collective-permute-start.14
  366.4 1.3 collective-permute-start.15
  367.8 0.3 collective-permute-done.14
  368.1 3.8 collective-permute-done.15
  371.9 0.5 maximum_maximum_fusion.3
  372.4 35.3 %fusion = f32[1,512,6,12,6]{1,0,4,3,2:T(1,128)S(1)} fusion(bf16[2,2,512,512,3,3,3]{3,2,6,5,4,1,0:T(8,128)(2,1)} %param.20, bf16[1,512,8,14,8]{1,3,4,2,0:T(8,128)(2,1)S(1)} %maximum_maximum_fusion.3), kind=kOutput, calls=%fused_computation | convolution fusion | flops 6115295232 | bytes 15958016 | tf_op jit(solution)/shard_map/conv_general_dilated | solution.py:51
  408.1 4.3 collective-permute-start.16
  412.4 2.0 collective-permute-start.17
  414.4 3.7 collective-permute-done.17
  418.3 2.6 collective-permute-start.18
  420.9 1.3 collective-permute-start.19
  422.5 3.8 collective-permute-done.19
  426.3 0.4 maximum_bitcast_fusion
  426.7 0.4 copy.69
  427.2 3.1 broadcast_in_dim.24
  430.4 8.8 %broadcast_in_dim.27 = bf16[1,512,6,28,16]{1,0,4,3,2:T(2,128)(2,1)} reshape(bf16[512,6,28,8,2]{0,4,3,2,1:T(2,128)(2,1)S(1)} %broadcast_in_dim.24) | data formatting | bytes 5505024 | tf_op jit(solution)/shard_map/broadcast_in_dim | solution.py:55
  439.2 54.7 %fusion.12 = f32[1,512,6,24,12]{1,0,4,3,2:T(1,128)S(1)} fusion(bf16[1,512,6,28,16]{1,0,4,3,2:T(2,128)(2,1)} %broadcast_in_dim.27, bf16[512,512,3,3]{1,0,3,2:T(8,128)(2,1)} %param.22), kind=kOutput, calls=%fused_computation.12 | convolution fusion | flops 8153726976 | bytes 11010048 | tf_op jit(solution)/shard_map/conv_general_dilated | solution.py:59
  494.0 2.2 fusion.14
  (111 shorter events, 6.3 us)
Async XLA Ops:
  0.0 57.4 %copy-start = (bf16[1,16,6,12,6]{3,1,4,2,0:T(8,128)(2,1)S(1)}, bf16[1,16,6,12,6]{3,1,4,2,0:T(8,128)(2,1)}, u32[]{:S(2)}) copy-start(bf16[1,16,6,12,6]{3,1,4,2,0:T(8,128)(2,1)} %param.13) | copy-start | bytes 41476
  57.3 1.6 copy-start.19
  59.5 11.7 %copy-start.12 = (f32[2,2,512]{2,1,0:T(2,128)S(1)}, f32[2,2,512]{2,1,0:T(2,128)}, u32[]{:S(2)}) copy-start(f32[2,2,512]{2,1,0:T(2,128)} %param.21) | copy-start | bytes 24580
  59.6 4.4 collective-permute-start
  61.6 5.7 %collective-permute-start.1 = (bf16[1,512,6,1,6]{1,3,4,2,0:T(2,128)(2,1)S(1)}, bf16[1,512,6,1,6]{1,3,4,2,0:T(2,128)(2,1)S(1)}, u32[]{:S(2)}, u32[]{:S(2)}) collective-permute-start(bf16[1,512,6,1,6]{1,3,4,2,0:T(2,128)(2,1)S(1)} %get-tuple-element.33), channel_id=1, source_target_pairs={{1,0},{2,1},{3,2},{4,3},{5,4},{6,5},{7,6},{9,8},{10,9},{11,10},{12... | collective-permute-start | bytes 110600 | tf_op jit(solution)/shard_map/ppermute | solution.py:27
  67.4 4.4 collective-permute-start.2
  69.8 5.4 %collective-permute-start.3 = (bf16[1,512,6,14,1]{1,3,4,2,0:T(8,128)(2,1)S(1)}, bf16[1,512,6,14,1]{1,3,4,2,0:T(8,128)(2,1)S(1)}, u32[]{:S(2)}, u32[]{:S(2)}) collective-permute-start(bf16[1,512,6,14,1]{1,3,4,2,0:T(8,128)(2,1)S(1)} %get-tuple-element.23), channel_id=1, source_target_pairs={{8,0},{16,8},{24,16},{9,1},{17,9},{25,17},{10,2},{18,10},{26,18},{... | collective-permute-start | bytes 258056 | tf_op jit(solution)/shard_map/ppermute | solution.py:27
  75.8 81.6 %copy-start.6 = (bf16[2,2,16,512]{3,2,1,0:T(8,128)(2,1)S(1)}, bf16[2,2,16,512]{3,2,1,0:T(8,128)(2,1)}, u32[]{:S(2)}) copy-start(bf16[2,2,16,512]{3,2,1,0:T(8,128)(2,1)} %param.16) | copy-start | bytes 196612
  158.5 4.4 collective-permute-start.4
  160.7 5.7 %collective-permute-start.5 = (bf16[1,512,6,1,6]{1,3,4,2,0:T(2,128)(2,1)S(1)}, bf16[1,512,6,1,6]{1,3,4,2,0:T(2,128)(2,1)S(1)}, u32[]{:S(2)}, u32[]{:S(2)}) collective-permute-start(bf16[1,512,6,1,6]{1,3,4,2,0:T(2,128)(2,1)S(1)} %get-tuple-element.31), channel_id=1, source_target_pairs={{1,0},{2,1},{3,2},{4,3},{5,4},{6,5},{7,6},{9,8},{10,9},{11,10},{12... | collective-permute-start | bytes 110600 | tf_op jit(solution)/shard_map/ppermute | solution.py:27
  166.5 3.9 collective-permute-start.6
  168.7 5.4 %collective-permute-start.7 = (bf16[1,512,6,14,1]{1,3,4,2,0:T(8,128)(2,1)S(1)}, bf16[1,512,6,14,1]{1,3,4,2,0:T(8,128)(2,1)S(1)}, u32[]{:S(2)}, u32[]{:S(2)}) collective-permute-start(bf16[1,512,6,14,1]{1,3,4,2,0:T(8,128)(2,1)S(1)} %get-tuple-element.21), channel_id=1, source_target_pairs={{8,0},{16,8},{24,16},{9,1},{17,9},{25,17},{10,2},{18,10},{26,18},{... | collective-permute-start | bytes 258056 | tf_op jit(solution)/shard_map/ppermute | solution.py:27
  174.7 35.2 %copy-start.4 = (bf16[1,512,6,12,6]{1,4,3,2,0:T(8,128)(2,1)S(1)}, bf16[1,512,6,12,6]{1,4,3,2,0:T(8,128)(2,1)}, u32[]{:S(2)}) copy-start(bf16[1,512,6,12,6]{1,4,3,2,0:T(8,128)(2,1)} %param.12) | copy-start | bytes 1327108
  174.7 35.2 %copy-start.11 = (f32[1,1,512]{2,1,0:T(1,128)S(1)}, f32[1,1,512]{2,1,0:T(1,128)}, u32[]{:S(2)}) copy-start(f32[1,1,512]{2,1,0:T(1,128)} %get-tuple-element.35) | copy-start | bytes 6148
  209.8 46.2 %copy-start.15 = (f32[1,1,512]{2,1,0:T(1,128)S(1)}, f32[1,1,512]{2,1,0:T(1,128)}, u32[]{:S(2)}) copy-start(f32[1,1,512]{2,1,0:T(1,128)} %get-tuple-element.42) | copy-start | bytes 6148
  209.8 46.2 %copy-start.16 = (f32[1,1,512]{2,1,0:T(1,128)S(1)}, f32[1,1,512]{2,1,0:T(1,128)}, u32[]{:S(2)}) copy-start(f32[1,1,512]{2,1,0:T(1,128)} %get-tuple-element.46) | copy-start | bytes 6148
  209.8 46.2 %copy-start.17 = (f32[1,1,512]{2,1,0:T(1,128)S(1)}, f32[1,1,512]{2,1,0:T(1,128)}, u32[]{:S(2)}) copy-start(f32[1,1,512]{2,1,0:T(1,128)} %get-tuple-element.50) | copy-start | bytes 6148
  210.2 46.8 %copy-start.2 = (bf16[1,512,6,12,6]{1,3,4,2,0:T(8,128)(2,1)}, bf16[1,512,6,12,6]{1,3,4,2,0:T(8,128)(2,1)S(1)}, u32[]{:S(2)}) copy-start(bf16[1,512,6,12,6]{1,3,4,2,0:T(8,128)(2,1)S(1)} %get-tuple-element.13) | copy-start | bytes 1327108
  210.2 46.2 %copy-start.18 = (f32[1,1,512]{2,1,0:T(1,128)S(1)}, f32[1,1,512]{2,1,0:T(1,128)}, u32[]{:S(2)}) copy-start(f32[1,1,512]{2,1,0:T(1,128)} %get-tuple-element.41) | copy-start | bytes 6148
  257.2 4.4 collective-permute-start.8
  259.3 5.7 %collective-permute-start.9 = (bf16[1,512,6,1,6]{1,3,4,2,0:T(2,128)(2,1)S(1)}, bf16[1,512,6,1,6]{1,3,4,2,0:T(2,128)(2,1)S(1)}, u32[]{:S(2)}, u32[]{:S(2)}) collective-permute-start(bf16[1,512,6,1,6]{1,3,4,2,0:T(2,128)(2,1)S(1)} %get-tuple-element.29), channel_id=1, source_target_pairs={{1,0},{2,1},{3,2},{4,3},{5,4},{6,5},{7,6},{9,8},{10,9},{11,10},{12... | collective-permute-start | bytes 110600 | tf_op jit(solution)/shard_map/ppermute | solution.py:27
  265.1 3.9 collective-permute-start.10
  267.4 5.4 %collective-permute-start.11 = (bf16[1,512,6,14,1]{1,3,4,2,0:T(8,128)(2,1)S(1)}, bf16[1,512,6,14,1]{1,3,4,2,0:T(8,128)(2,1)S(1)}, u32[]{:S(2)}, u32[]{:S(2)}) collective-permute-start(bf16[1,512,6,14,1]{1,3,4,2,0:T(8,128)(2,1)S(1)} %get-tuple-element.19), channel_id=1, source_target_pairs={{8,0},{16,8},{24,16},{9,1},{17,9},{25,17},{10,2},{18,10},{26,18},{... | collective-permute-start | bytes 258056 | tf_op jit(solution)/shard_map/ppermute | solution.py:27
  273.3 35.5 %copy-start.5 = (f32[1,1,512]{2,1,0:T(1,128)S(1)}, f32[1,1,512]{2,1,0:T(1,128)}, u32[]{:S(2)}) copy-start(f32[1,1,512]{2,1,0:T(1,128)} %get-tuple-element.37) | copy-start | bytes 6148
  273.3 81.6 %copy-start.7 = (f32[1,1,512]{2,1,0:T(1,128)S(1)}, f32[1,1,512]{2,1,0:T(1,128)}, u32[]{:S(2)}) copy-start(f32[1,1,512]{2,1,0:T(1,128)} %get-tuple-element.45) | copy-start | bytes 6148
  273.3 81.6 %copy-start.8 = (f32[1,1,512]{2,1,0:T(1,128)S(1)}, f32[1,1,512]{2,1,0:T(1,128)}, u32[]{:S(2)}) copy-start(f32[1,1,512]{2,1,0:T(1,128)} %get-tuple-element.49) | copy-start | bytes 6148
  273.3 81.6 %copy-start.10 = (f32[1,1,512]{2,1,0:T(1,128)S(1)}, f32[1,1,512]{2,1,0:T(1,128)}, u32[]{:S(2)}) copy-start(f32[1,1,512]{2,1,0:T(1,128)} %get-tuple-element.53) | copy-start | bytes 6148
  354.9 0.7 copy-start.14
  356.2 4.4 collective-permute-start.12
  358.4 5.7 %collective-permute-start.13 = (bf16[1,512,6,1,6]{1,3,4,2,0:T(2,128)(2,1)S(1)}, bf16[1,512,6,1,6]{1,3,4,2,0:T(2,128)(2,1)S(1)}, u32[]{:S(2)}, u32[]{:S(2)}) collective-permute-start(bf16[1,512,6,1,6]{1,3,4,2,0:T(2,128)(2,1)S(1)} %get-tuple-element.27), channel_id=1, source_target_pairs={{1,0},{2,1},{3,2},{4,3},{5,4},{6,5},{7,6},{9,8},{10,9},{11,10},{12... | collective-permute-start | bytes 110600 | tf_op jit(solution)/shard_map/ppermute | solution.py:27
  364.2 3.9 collective-permute-start.14
  366.4 5.4 %collective-permute-start.15 = (bf16[1,512,6,14,1]{1,3,4,2,0:T(8,128)(2,1)S(1)}, bf16[1,512,6,14,1]{1,3,4,2,0:T(8,128)(2,1)S(1)}, u32[]{:S(2)}, u32[]{:S(2)}) collective-permute-start(bf16[1,512,6,14,1]{1,3,4,2,0:T(8,128)(2,1)S(1)} %get-tuple-element.17), channel_id=1, source_target_pairs={{8,0},{16,8},{24,16},{9,1},{17,9},{25,17},{10,2},{18,10},{26,18},{... | collective-permute-start | bytes 258056 | tf_op jit(solution)/shard_map/ppermute | solution.py:27
  372.4 35.4 %copy-start.3 = (bf16[1,512,6,12,6]{1,3,4,2,0:T(8,128)(2,1)S(1)}, bf16[1,512,6,12,6]{1,3,4,2,0:T(8,128)(2,1)}, u32[]{:S(2)}) copy-start(bf16[1,512,6,12,6]{1,3,4,2,0:T(8,128)(2,1)} %copy-done.2) | copy-start | bytes 1327108
  372.4 35.4 %copy-start.9 = (f32[1,1,512]{2,1,0:T(1,128)S(1)}, f32[1,1,512]{2,1,0:T(1,128)}, u32[]{:S(2)}) copy-start(f32[1,1,512]{2,1,0:T(1,128)} %get-tuple-element.34) | copy-start | bytes 6148
  408.1 6.3 %collective-permute-start.16 = (bf16[1,512,6,1,6]{1,3,4,2,0:T(2,128)(2,1)S(1)}, bf16[1,512,6,1,6]{1,3,4,2,0:T(2,128)(2,1)S(1)}, u32[]{:S(2)}, u32[]{:S(2)}) collective-permute-start(bf16[1,512,6,1,6]{1,3,4,2,0:T(2,128)(2,1)S(1)} %get-tuple-element.24), channel_id=1, source_target_pairs={{0,1},{1,2},{2,3},{3,4},{4,5},{5,6},{6,7},{8,9},{9,10},{10,11},{11... | collective-permute-start | bytes 110600 | tf_op jit(solution)/shard_map/ppermute | solution.py:26
  412.4 5.7 %collective-permute-start.17 = (bf16[1,512,6,1,6]{1,3,4,2,0:T(2,128)(2,1)S(1)}, bf16[1,512,6,1,6]{1,3,4,2,0:T(2,128)(2,1)S(1)}, u32[]{:S(2)}, u32[]{:S(2)}) collective-permute-start(bf16[1,512,6,1,6]{1,3,4,2,0:T(2,128)(2,1)S(1)} %get-tuple-element.25), channel_id=1, source_target_pairs={{1,0},{2,1},{3,2},{4,3},{5,4},{6,5},{7,6},{9,8},{10,9},{11,10},{12... | collective-permute-start | bytes 110600 | tf_op jit(solution)/shard_map/ppermute | solution.py:27
  418.3 4.2 collective-permute-start.18
  420.9 5.4 %collective-permute-start.19 = (bf16[1,512,6,14,1]{1,3,4,2,0:T(8,128)(2,1)S(1)}, bf16[1,512,6,14,1]{1,3,4,2,0:T(8,128)(2,1)S(1)}, u32[]{:S(2)}, u32[]{:S(2)}) collective-permute-start(bf16[1,512,6,14,1]{1,3,4,2,0:T(8,128)(2,1)S(1)} %get-tuple-element.15), channel_id=1, source_target_pairs={{8,0},{16,8},{24,16},{9,1},{17,9},{25,17},{10,2},{18,10},{26,18},{... | collective-permute-start | bytes 258056 | tf_op jit(solution)/shard_map/ppermute | solution.py:27
  439.2 54.8 %copy-start.13 = (f32[512]{0:T(512)S(1)}, f32[512]{0:T(512)}, u32[]{:S(2)}) copy-start(f32[512]{0:T(512)} %param.23) | copy-start | bytes 6148
  494.0 2.2 copy-start.1
where the time goes:
time: 501 us; the launch traced here: 496 us
  matrix products  201 us (40%)
  blocking collectives  185 us (37%)
  starting transfers between devices  42.1 us (8%)
  waiting for transfers between devices  37 us (7%)
  local copies, waits for them, and re-layouts  21.2 us (4%)
  other arithmetic  8.78 us (2%)
    psum x4, blocking collectives, group_norm(): total_stats = lax.psum(local_stats, ('sh', 'sw'))  185 us
    conv_general_dilated x4, matrix products, causal_conv(): lax.conv_general_dilated(padded, weight, (1, 1, 1), 'VALID', dimension_nu...  141 us
    conv_general_dilated x1, matrix products, upsample_conv(): lax.conv_general_dilated(cropped, weight[:, :, None], (1, 1, 1), 'VALID',...  54.7 us
    ppermute x10, waiting for transfers between devices, edge_exchange(): lax.ppermute(head, axis_name, [(i + 1, i) for i in range(n_dev - 1)])  35.8 us
    ppermute x10, starting transfers between devices, edge_exchange(): lax.ppermute(tail, axis_name, [(i, i + 1) for i in range(n_dev - 1)])  24.4 us
    ppermute x10, starting transfers between devices, edge_exchange(): lax.ppermute(head, axis_name, [(i + 1, i) for i in range(n_dev - 1)])  17.7 us
    broadcast_in_dim x3, local copies, waits for them, and re-layouts, upsample_conv(): upsampled = jnp.repeat(jnp.repeat(bordered, 2, axis=3), 2, axis=4)  12.1 us
  transfers between devices with their start and end apart: 20, of which 14 were waited for; matrix products, arithmetic and copies ran while one was open for 0% of the time, Pallas kernels for 0%

commit v1 on v0

v1 whole, which is shorter than its diff:
```python
import functools

import jax
import jax.numpy as jnp
from jax import lax
from jax.experimental import pallas as pl
from jax.experimental.pallas import tpu as pltpu
from jax.sharding import PartitionSpec as P

NUM_GROUPS = 32
GN_EPSILON = 1e-6
LANES = 128
SLOTS = 8
RING = 4
MESH = pl.DeviceIdType.MESH
F32 = jnp.float32
BF16 = jnp.bfloat16


def limbs(values):
    high = values.astype(BF16)
    rest = values - high.astype(F32)
    mid = rest.astype(BF16)
    low = (rest - mid.astype(F32)).astype(BF16)
    n = values.shape[0]
    pad = jnp.zeros((16 - 3 * n, values.shape[1]), F32)
    return jnp.concatenate([high.astype(F32), mid.astype(F32), low.astype(F32), pad], axis=0).astype(BF16)


def contract_lanes(a, b):
    return lax.dot_general(a, b, (((1,), (1,)), ((), ())), preferred_element_type=F32)


def block_kernel(dims, x_ref, z_ref, gain_ref, shift_ref, zyw_ref, zyb_ref, zbw_ref, zbb_ref, cw_ref, cb_ref, uw_ref, ub_ref, y_ref,
                 ex, colx, cols, zx, zcolx, zcols, zext, stat_all, group, wyb, yb, xk, acc, hidden, wbuf, prod, xu,
                 wsem, hsend, hrecv, zsend, zrecv, ssend, srecv):
    n_sh, n_sw, n_frame, n_row, n_col, n_chan, n_conv = dims
    main = n_col * SLOTS
    wide = (n_col + 2) * SLOTS
    n_dev = n_sh * n_sw
    count = (n_chan // NUM_GROUPS) * n_frame * n_row * n_col * n_dev
    sh = lax.axis_index("sh")
    sw = lax.axis_index("sw")
    me = sw * n_sh + sh
    up, down = (sh + n_sh - 1) % n_sh, (sh + 1) % n_sh
    left, right = (sw + n_sw - 1) % n_sw, (sw + 1) % n_sw

    def weight_start(q):
        slot = q % RING
        for tap in range(9):
            dst = wbuf.at[slot, :, pl.ds(tap * n_chan, n_chan)]

            @pl.when(q < 3 * n_conv)
            def _():
                pltpu.make_async_copy(cw_ref.at[jnp.minimum(q, 3 * n_conv - 1), tap], dst, wsem.at[slot]).start()

            @pl.when(q == 3 * n_conv)
            def _():
                pltpu.make_async_copy(uw_ref.at[tap], dst, wsem.at[slot]).start()

    def weight_wait(q):
        slot = q % RING
        pltpu.make_async_copy(wbuf.at[slot], wbuf.at[slot], wsem.at[slot]).wait()

    for q in range(RING):
        weight_start(jnp.int32(q))

    barrier = pltpu.get_barrier_semaphore()

    def peer_of(k):
        target = (me + k) % n_dev
        return {"sh": target % n_sh, "sw": target // n_sh}

    @pl.loop(1, n_dev)
    def _(k):
        pl.semaphore_signal(barrier, inc=1, device_id=peer_of(k), device_id_type=MESH)

    def halo_copies(rows, recv_cols, send_cols, send_sem, recv_sem):
        table = [
            (rows.at[1], rows.at[n_row + 1], {"sh": up}),
            (rows.at[n_row], rows.at[0], {"sh": down}),
            (send_cols.at[0], recv_cols.at[1, pl.ds(1, n_row)], {"sw": left}),
            (send_cols.at[1], recv_cols.at[0, pl.ds(1, n_row)], {"sw": right}),
            (send_cols.at[0, 0], recv_cols.at[1, n_row + 1], {"sh": up, "sw": left}),
            (send_cols.at[1, 0], recv_cols.at[0, n_row + 1], {"sh": up, "sw": right}),
            (send_cols.at[0, n_row - 1], recv_cols.at[1, 0], {"sh": down, "sw": left}),
            (send_cols.at[1, n_row - 1], recv_cols.at[0, 0], {"sh": down, "sw": right}),
        ]
        return [pltpu.make_async_remote_copy(src_ref=src, dst_ref=dst, send_sem=send_sem.at[k], recv_sem=recv_sem.at[k],
                                             device_id=where, device_id_type=MESH) for k, (src, dst, where) in enumerate(table)]

    def block_halo(par):
        return halo_copies(ex.at[par], colx.at[par], cols.at[par], hsend.at[par], hrecv.at[par])

    def stats_send(par, sums):
        parts = jnp.dot(limbs(sums), group[...], preferred_element_type=F32)
        mine = parts[0:2] + parts[2:4] + parts[4:6]
        stat_all[par, me] = jnp.concatenate([mine, jnp.zeros((6, LANES), F32)], axis=0)

        @pl.loop(1, n_dev)
        def _(k):
            pltpu.make_async_remote_copy(src_ref=stat_all.at[par, me], dst_ref=stat_all.at[par, me], send_sem=ssend.at[par],
                                         recv_sem=srecv.at[par], device_id=peer_of(k), device_id_type=MESH).start()

    def stats_wait(par):
        several = stat_all.at[par, pl.ds(0, n_dev - 1)]
        pltpu.make_async_copy(several, several, srecv.at[par]).wait()
        pltpu.make_async_copy(several, several, ssend.at[par]).wait()

    chan = lax.broadcasted_iota(jnp.int32, (n_chan, LANES), 0)
    first = lax.broadcasted_iota(jnp.int32, (n_chan, LANES), 1) * (n_chan // NUM_GROUPS)
    member = (chan >= first) & (chan < first + n_chan // NUM_GROUPS)
    group[...] = jnp.where(member, 1.0, 0.0).astype(BF16)
    wyb[...] = jnp.zeros_like(wyb)

    def tile_sums(values):
        total = values[0:SLOTS]
        for c in range(1, n_col):
            total = total + values[c * SLOTS:(c + 1) * SLOTS]
        return total

    def sums_of(first_sum, second_sum):
        return jnp.concatenate([jnp.sum(first_sum, axis=0, keepdims=True), jnp.sum(second_sum, axis=0, keepdims=True)], axis=0)

    zero_sums = (jnp.zeros((SLOTS, n_chan), F32), jnp.zeros((SLOTS, n_chan), F32))

    def load_row(r, carry):
        raw = x_ref[r]
        values = raw.astype(F32)
        ex[0, r + 1] = raw
        hidden[r] = raw
        cols[0, 0, r] = values[0:SLOTS].astype(BF16)
        cols[0, 1, r] = values[main - SLOTS:main].astype(BF16)
        latent = z_ref[r]
        wide_latent = latent.astype(F32)
        zx[r + 1] = latent
        zcols[0, r] = wide_latent[0:SLOTS].astype(BF16)
        zcols[1, r] = wide_latent[main - SLOTS:main].astype(BF16)
        return carry[0] + tile_sums(values), carry[1] + tile_sums(values * values)

    start_sums = lax.fori_loop(0, n_row, load_row, zero_sums)

    pl.semaphore_wait(barrier, n_dev - 1)
    for copy in block_halo(0):
        copy.start()
    z_copies = halo_copies(zx, zcolx, zcols, zsend, zrecv)
    for copy in z_copies:
        copy.start()
    stats_send(0, sums_of(*start_sums))
    for copy in z_copies:
        copy.wait()

    @pl.loop(0, n_row + 2)
    def _(r):
        zext[r] = jnp.concatenate([zcolx[0, r].astype(F32), zx[r].astype(F32), zcolx[1, r].astype(F32)], axis=0).astype(BF16)

    row_of = lax.broadcasted_iota(jnp.int32, (wide, n_chan), 0)
    slot_of = lax.broadcasted_iota(jnp.int32, (n_col + 2, SLOTS, n_chan), 1)
    first_valid = jnp.where(sw == 0, SLOTS, 0)
    last_valid = jnp.where(sw == n_sw - 1, wide - SLOTS, wide)

    def inside(r):
        beyond = ((r == 0) & (sh == 0)) | ((r == n_row + 1) & (sh == n_sh - 1))
        end = jnp.where(beyond, 0, last_valid)
        return (row_of >= first_valid) & (row_of < end)

    def wide_row(par, r):
        return jnp.concatenate([colx[par, 0, r].astype(F32), ex[par, r].astype(F32), colx[par, 1, r].astype(F32)], axis=0)

    frame_of = lax.broadcasted_iota(jnp.int32, (n_col, SLOTS, n_chan), 1).reshape(main, n_chan)

    def conv_step(i, _):
        par = i % 2
        after = (i + 1) % 2

        wyb[0:zyw_ref.shape[1], 0:n_chan] = zyw_ref[i]
        wyb[0:zyw_ref.shape[1], n_chan:2 * n_chan] = zbw_ref[i]
        maps = jnp.dot(zext[...].reshape((n_row + 2) * wide, LANES), wyb[...], preferred_element_type=F32)
        map_bias = jnp.concatenate([zyb_ref[i], zbb_ref[i]], axis=1)
        yb[...] = (maps + map_bias).reshape(n_row + 2, wide, 2 * n_chan)

        stats_wait(par)
        total = stat_all[par, 0]
        for d in range(1, n_dev):
            total = total + stat_all[par, d]
        group_mean = total[0:1] / count
        group_var = jnp.maximum(total[1:2] / count - group_mean * group_mean, 0.0)
        both = jnp.concatenate([group_mean, lax.rsqrt(group_var + GN_EPSILON)], axis=0)
        spread = contract_lanes(limbs(both), group[...])
        chan_both = spread[0:2] + spread[2:4] + spread[4:6]
        mean = chan_both[0:1]
        scale = chan_both[1:2] * gain_ref[i]
        shift = shift_ref[i]
        for copy in block_halo(par):
            copy.wait()

        @pl.loop(0, n_row + 2)
        def _(r):
            normed = (wide_row(par, r) - mean) * scale + shift
            mixed = normed * yb[r, :, 0:n_chan] + yb[r, :, n_chan:2 * n_chan]
            act = jnp.where(inside(r), mixed * jax.nn.sigmoid(mixed), 0.0)
            taps = act.reshape(n_col + 2, SLOTS, n_chan)
            for kt in (2, 1, 0):
                for dw in range(3):
                    xk[kt, r, :, dw * n_chan:(dw + 1) * n_chan] = taps[dw:dw + n_col].reshape(main, n_chan).astype(BF16)
                if kt > 0:
                    taps = jnp.where(slot_of == 0, taps, pltpu.roll(taps, 1, 1))

        @pl.loop(0, 3)
        def _(kt):
            q = i * 3 + kt
            weight_wait(q)
            lhs = jnp.concatenate([xk[kt, dh:dh + n_row].reshape(n_row * main, 3 * n_chan) for dh in range(3)], axis=1)
            part = contract_lanes(lhs, wbuf[q % RING])

            @pl.when(kt == 0)
            def _():
                acc[...] = part

            @pl.when(kt > 0)
            def _():
                acc[...] = acc[...] + part

            @pl.when(q + RING <= 3 * n_conv)
            def _():
                weight_start(q + RING)

        bias = cb_ref[i]
        second = i % 2 == 1

        def finish_row(r, carry):
            conv = (acc[pl.ds(pl.multiple_of(r * main, main), main), :] + bias).astype(BF16).astype(F32)
            old = hidden[r].astype(F32)
            value = jnp.where(second, old + conv, conv).astype(BF16).astype(F32)
            value = jnp.where(frame_of < n_frame, value, 0.0)
            hidden[r] = jnp.where(second, value, old).astype(BF16)
            ex[after, r + 1] = value.astype(BF16)
            cols[after, 0, r] = value[0:SLOTS].astype(BF16)
            cols[after, 1, r] = value[main - SLOTS:main].astype(BF16)
            return carry[0] + tile_sums(value), carry[1] + tile_sums(value * value)

        sums = lax.fori_loop(0, n_row, finish_row, zero_sums)
        for copy in block_halo(after):
            copy.start()

        @pl.when(i < n_conv - 1)
        def _():
            stats_send(after, sums_of(*sums))

        return 0

    lax.fori_loop(0, n_conv, conv_step, 0)

    par = n_conv % 2
    for copy in block_halo(par):
        copy.wait()

    @pl.loop(0, n_row + 2)
    def _(r):
        xu[r] = jnp.where(inside(r), wide_row(par, r), 0.0).astype(BF16)

    last = 3 * n_conv
    weight_wait(last)

    @pl.loop(0, 3)
    def _(dy):
        begin = jnp.minimum(dy, 1)
        lhs = xu[pl.ds(begin, n_row + 1)].reshape((n_row + 1) * wide, n_chan)
        for dx in range(3):
            w = wbuf[last % RING, :, pl.ds(pl.multiple_of((dy * 3 + dx) * n_chan, n_chan), n_chan)]
            prod[dy, :, :, dx * n_chan:(dx + 1) * n_chan] = contract_lanes(lhs, w).reshape(n_row + 1, wide, n_chan)

    up_bias = ub_ref[...]

    @pl.loop(0, n_row)
    def _(r):
        for py in range(2):
            def of(dx, lo):
                at = (slice(lo, lo + main), slice(dx * n_chan, (dx + 1) * n_chan))
                return prod[(0, r + py) + at] + prod[(1, r) + at] + prod[(2, r + py) + at]

            middle = of(1, SLOTS) + up_bias
            phases = [of(0, 0) + middle + of(2, SLOTS), of(0, SLOTS) + middle + of(2, 2 * SLOTS)]
            tiles = [phases[px][c * SLOTS:(c + 1) * SLOTS] for c in range(n_col) for px in range(2)]
            y_ref[2 * r + py] = jnp.concatenate(tiles, axis=0).astype(BF16)


def solution(mesh):
    n_sh = mesh.shape["sh"]
    n_sw = mesh.shape["sw"]

    def local_step(features, latent, gn_gain, gn_bias, zy_weight, zy_bias, zb_weight, zb_bias, conv_weight, conv_bias, up_weight, up_bias):
        _, n_chan, n_frame, n_row, n_col = features.shape
        n_latent = latent.shape[1]
        n_conv = gn_gain.shape[0] * gn_gain.shape[1]
        main = n_col * SLOTS
        wide = main + 2 * SLOTS
        n_dev = n_sh * n_sw

        def tiles_of(values, lanes):
            moved = jnp.transpose(values[0], (2, 3, 1, 0))
            padded = jnp.pad(moved, ((0, 0), (0, 0), (0, SLOTS - n_frame), (0, lanes - values.shape[1])))
            return padded.reshape(n_row, main, lanes)

        vector = lambda values: values.reshape(n_conv, 1, n_chan)
        small = lambda values: values.reshape(n_conv, n_latent, n_chan)
        taps = jnp.transpose(conv_weight, (0, 1, 4, 5, 6, 2, 3)).reshape(3 * n_conv, 9, n_chan, n_chan)
        up_taps = jnp.transpose(up_weight, (2, 3, 0, 1)).reshape(9, n_chan, n_chan)
        dims = (n_sh, n_sw, n_frame, n_row, n_col, n_chan, n_conv)
        vmem = pl.BlockSpec(memory_space=pltpu.VMEM)
        hbm = pl.BlockSpec(memory_space=pl.ANY)
        dma = pltpu.SemaphoreType.DMA
        rows = n_row + 2
        result = pl.pallas_call(
            functools.partial(block_kernel, dims),
            out_shape=jax.ShapeDtypeStruct((2 * n_row, 2 * main, n_chan), BF16),
            in_specs=[vmem] * 8 + [hbm, vmem, hbm, vmem],
            out_specs=vmem,
            scratch_shapes=[
                pltpu.VMEM((2, rows, main, n_chan), BF16),
                pltpu.VMEM((2, 2, rows, SLOTS, n_chan), BF16),
                pltpu.VMEM((2, 2, n_row, SLOTS, n_chan), BF16),
                pltpu.VMEM((rows, main, LANES), BF16),
                pltpu.VMEM((2, rows, SLOTS, LANES), BF16),
                pltpu.VMEM((2, n_row, SLOTS, LANES), BF16),
                pltpu.VMEM((rows, wide, LANES), BF16),
                pltpu.VMEM((2, n_dev, 8, LANES), F32),
                pltpu.VMEM((n_chan, LANES), BF16),
                pltpu.VMEM((LANES, 2 * n_chan), BF16),
                pltpu.VMEM((rows, wide, 2 * n_chan), F32),
                pltpu.VMEM((3, rows, main, 3 * n_chan), BF16),
                pltpu.VMEM((n_row * main, n_chan), F32),
                pltpu.VMEM((n_row, main, n_chan), BF16),
                pltpu.VMEM((RING, n_chan, 9 * n_chan), BF16),
                pltpu.VMEM((3, n_row + 1, wide, 3 * n_chan), F32),
                pltpu.VMEM((rows, wide, n_chan), BF16),
                dma((RING,)),
                dma((2, 8)),
                dma((2, 8)),
                dma((8,)),
                dma((8,)),
                dma((2,)),
                dma((2,)),
            ],
            compiler_params=pltpu.CompilerParams(collective_id=0, has_side_effects=True, vmem_limit_bytes=64 * 1024 * 1024 - 65536 - 4096),
            name="decoder_block",
        )(tiles_of(features, n_chan), tiles_of(latent, LANES), vector(gn_gain), vector(gn_bias), small(zy_weight), vector(zy_bias),
          small(zb_weight), vector(zb_bias), taps, vector(conv_bias), up_taps, up_bias.reshape(1, n_chan))
        frames = result.reshape(2 * n_row, 2 * n_col, SLOTS, n_chan)[:, :, :n_frame]
        return jnp.transpose(frames, (3, 2, 0, 1))[None]

    data_spec = P("dp", None, None, "sh", "sw")
    return jax.shard_map(local_step, mesh=mesh, in_specs=(data_spec, data_spec) + (P(),) * 10, out_specs=data_spec, check_vma=False)
```

time: 501 us -> 108 us (0.22)
  matrix products: 201 us -> 0 us
  blocking collectives: 185 us -> 0 us
  Pallas kernels: 0 us -> 93.4 us
  starting transfers between devices: 42.1 us -> 0 us
  waiting for transfers between devices: 37 us -> 0 us
  other arithmetic: 8.78 us -> 0 us
  local copies, waits for them, and re-layouts: 21.2 us -> 14.6 us
    conv_general_dilated x5 -> x0, matrix products: 196 us -> none  [the longest x4 141 us: causal_conv(): lax.conv_general_dilated(padded, weight, (1, 1, 1), 'VALID', dimension_nu...]
    psum x4 -> x0, blocking collectives: 185 us -> none  [group_norm(): total_stats = lax.psum(local_stats, ('sh', 'sw'))]
    pallas_call x0 -> x1, Pallas kernels: none -> 93.4 us  [local_step(): pl.pallas_call(functools.partial(block_kernel, dims), out_shape=jax.Shape...]
    ppermute x20 -> x0, starting transfers between devices: 42.1 us -> none  [the longest x10 24.4 us: edge_exchange(): lax.ppermute(tail, axis_name, [(i, i + 1) for i in range(n_dev - 1)])]
    ppermute x20 -> x0, waiting for transfers between devices: 37 us -> none  [the longest x10 35.8 us: edge_exchange(): lax.ppermute(head, axis_name, [(i + 1, i) for i in range(n_dev - 1)])]
    broadcast_in_dim x3 -> x0, local copies, waits for them, and re-layouts: 12.1 us -> none  [upsample_conv(): upsampled = jnp.repeat(jnp.repeat(bordered, 2, axis=3), 2, axis=4)]
    reshape x0 -> x7, local copies, waits for them, and re-layouts: none -> 8.17 us  [the longest x5 6.53 us: local_step(): vector = lambda values: values.reshape(n_conv, 1, n_chan)]
    slice x10 -> x0, local copies, waits for them, and re-layouts: 6.66 us -> none  [the longest x2 2.74 us: local_step(): normed = group_norm(branch, gn_gain[block, slot], gn_bias[block, slot])]
  transfers between devices with their start and end apart: 20 -> 0, of which waited for: 14 -> 0; matrix products, arithmetic and copies ran while one was open for 0% -> 0% of each run, Pallas kernels for 0% -> 0%
where the time goes in v1:
time: 108 us
  Pallas kernels  93.4 us (86%)
  local copies, waits for them, and re-layouts  14.6 us (14%)
    pallas_call x1, Pallas kernels, local_step(): pl.pallas_call(functools.partial(block_kernel, dims), out_shape=jax.Shape...  93.4 us
    reshape x5, local copies, waits for them, and re-layouts, local_step(): vector = lambda values: values.reshape(n_conv, 1, n_chan)  6.53 us
    unnamed x3, local copies, waits for them, and re-layouts  6.45 us

profile of v1, /device:TPU:97, one launch (start us, length us, event | category | flops | bytes accessed | tf_op | source)
XLA Modules:
  0.0 108.0 jit_solution(3219182988279893955)
XLA Ops:
  0.0 1.3 %reshape.41.gain_ref = f32[4,1,512]{2,1,0:T(1,128)} reshape(f32[2,2,512]{2,1,0:T(2,128)} %param.14) | data formatting | bytes 16384 | tf_op jit(solution)/shard_map/reshape | solution.py:305
  1.3 1.3 %reshape.42.shift_ref = f32[4,1,512]{2,1,0:T(1,128)} reshape(f32[2,2,512]{2,1,0:T(2,128)} %param.15) | data formatting | bytes 16384 | tf_op jit(solution)/shard_map/reshape | solution.py:305
  2.6 1.3 %reshape.44.zyb_ref = f32[4,1,512]{2,1,0:T(1,128)} reshape(f32[2,2,512]{2,1,0:T(2,128)} %param.17) | data formatting | bytes 16384 | tf_op jit(solution)/shard_map/reshape | solution.py:305
  3.9 1.3 %reshape.46.zbb_ref = f32[4,1,512]{2,1,0:T(1,128)} reshape(f32[2,2,512]{2,1,0:T(2,128)} %param.19) | data formatting | bytes 16384 | tf_op jit(solution)/shard_map/reshape | solution.py:305
  5.2 1.3 %reshape.48.cb_ref = f32[4,1,512]{2,1,0:T(1,128)} reshape(f32[2,2,512]{2,1,0:T(2,128)} %param.21) | data formatting | bytes 16384 | tf_op jit(solution)/shard_map/reshape | solution.py:305
  6.5 1.3 %copy.18 = bf16[12,6,6,16]{3,2,1,0:T(8,128)(2,1)S(1)} copy(bf16[12,6,6,16]{0,3,1,2:T(8,128)(2,1)} %bitcast.30) | data formatting | bytes 27648
  7.8 0.7 pad_bitcast_fusion.1.z_ref
  8.5 1.3 %copy.17 = bf16[12,6,6,512]{3,2,1,0:T(8,128)(2,1)S(1)} copy(bf16[12,6,6,512]{3,1,0,2:T(8,128)(2,1)} %bitcast.29) | data formatting | bytes 884736
  9.9 0.9 pad_bitcast_fusion.x_ref
  10.8 93.4 %decoder_block.1 = bf16[24,96,512]{2,1,0:T(8,128)(2,1)} custom-call(bf16[12,48,512]{2,1,0:T(8,128)(2,1)} %pad_bitcast_fusion.x_ref, bf16[12,48,128]{2,1,0:T(8,128)(2,1)} %pad_bitcast_fusion.1.z_ref, f32[4,1,512]{2,1,0:T(1,128)} %reshape.41.gain_ref, f32[4,1,512]{2,1,0:T(1,128)} %reshape.42.shift_ref, bf16[4,16,512]{2,1,0:T(8,128)(2,1)} %bitcast.31, ...), custom_call_target="tpu_custom_call" | custom-call | tf_op jit(solution)/shard_map/decoder_block/pallas_call | solution.py:314
  104.2 3.8 %copy.20 = bf16[24,12,6,512]{3,0,1,2:T(8,128)(2,1)} copy(bf16[24,12,6,512]{3,2,1,0:T(8,128)(2,1)} %bitcast.27) | data formatting | bytes 3538944

commit v2 on v1

v2 whole, which is shorter than its diff:
```python
import functools

import jax
import jax.numpy as jnp
from jax import lax
from jax.experimental import pallas as pl
from jax.experimental.pallas import tpu as pltpu
from jax.sharding import PartitionSpec as P

NUM_GROUPS = 32
GN_EPSILON = 1e-6
LANES = 128
SLOTS = 8
RING = 9
MESH = pl.DeviceIdType.MESH
F32 = jnp.float32
BF16 = jnp.bfloat16


def limbs(values):
    high = values.astype(BF16)
    rest = values - high.astype(F32)
    mid = rest.astype(BF16)
    low = (rest - mid.astype(F32)).astype(BF16)
    n = values.shape[0]
    pad = jnp.zeros((16 - 3 * n, values.shape[1]), F32)
    return jnp.concatenate([high.astype(F32), mid.astype(F32), low.astype(F32), pad], axis=0).astype(BF16)


def contract_lanes(a, b):
    return lax.dot_general(a, b, (((1,), (1,)), ((), ())), preferred_element_type=F32)


def block_kernel(dims, x_ref, z_ref, gain_ref, shift_ref, zyw_ref, zyb_ref, zbw_ref, zbb_ref, cw_ref, cb_ref, uw_ref, ub_ref, y_ref,
                 ex, colx, cols, zx, zcolx, zcols, zext, stat_all, group, wyb, yb, xk, acc, hidden, wbuf, prod, xt, zt,
                 wsem, hsend, hrecv, zsend, zrecv, ssend, srecv):
    n_sh, n_sw, n_frame, n_row, n_col, n_chan, n_conv = dims
    half = n_chan // 2
    main = n_col * SLOTS
    wide = (n_col + 2) * SLOTS
    n_dev = n_sh * n_sw
    per_group = n_chan // NUM_GROUPS
    count = per_group * n_frame * n_row * n_col * n_dev
    sh = lax.axis_index("sh")
    sw = lax.axis_index("sw")
    me = sw * n_sh + sh
    up, down = (sh + n_sh - 1) % n_sh, (sh + 1) % n_sh
    left, right = (sw + n_sw - 1) % n_sw, (sw + 1) % n_sw

    last_group = 6 * n_conv

    def weight_start(g):
        slot = g % RING
        source = (g // 6) * 3 + g % 3
        from_half = (g // 3) % 2
        for tap in range(9):
            dst = wbuf.at[slot, :, pl.ds(tap * half, half)]

            @pl.when(g < last_group)
            def _():
                lanes = pl.ds(pl.multiple_of(from_half * half, half), half)
                pltpu.make_async_copy(cw_ref.at[jnp.minimum(source, 3 * n_conv - 1), tap, :, lanes], dst, wsem.at[slot]).start()

            @pl.when((g >= last_group) & (g < last_group + 2))
            def _():
                lanes = pl.ds(pl.multiple_of(jnp.clip(g - last_group, 0, 1) * half, half), half)
                pltpu.make_async_copy(uw_ref.at[tap, :, lanes], dst, wsem.at[slot]).start()

    def weight_wait(g):
        slot = g % RING
        pltpu.make_async_copy(wbuf.at[slot], wbuf.at[slot], wsem.at[slot]).wait()

    @pl.loop(0, RING)
    def _(g):
        weight_start(g)

    barrier = pltpu.get_barrier_semaphore()
    peers = [{"sh": (sh + b) % n_sh, "sw": (sw + a) % n_sw} for a in range(n_sw) for b in range(n_sh)][1:]
    for peer in peers:
        pl.semaphore_signal(barrier, inc=1, device_id=peer, device_id_type=MESH)

    def halo_copies(rows, recv_cols, send_cols, send_sem, recv_sem):
        table = [
            (send_cols.at[0], recv_cols.at[1, pl.ds(1, n_row)], {"sw": left}),
            (send_cols.at[1], recv_cols.at[0, pl.ds(1, n_row)], {"sw": right}),
            (rows.at[1], rows.at[n_row + 1], {"sh": up}),
            (rows.at[n_row], rows.at[0], {"sh": down}),
            (send_cols.at[0, 0], recv_cols.at[1, n_row + 1], {"sh": up, "sw": left}),
            (send_cols.at[1, 0], recv_cols.at[0, n_row + 1], {"sh": up, "sw": right}),
            (send_cols.at[0, n_row - 1], recv_cols.at[1, 0], {"sh": down, "sw": left}),
            (send_cols.at[1, n_row - 1], recv_cols.at[0, 0], {"sh": down, "sw": right}),
        ]
        return [pltpu.make_async_remote_copy(src_ref=src, dst_ref=dst, send_sem=send_sem.at[k], recv_sem=recv_sem.at[k],
                                             device_id=where, device_id_type=MESH) for k, (src, dst, where) in enumerate(table)]

    def block_halo(par, h):
        return halo_copies(ex.at[par, h], colx.at[par, h], cols.at[par, h], hsend.at[par, h], hrecv.at[par, h])

    def stats_send(par, h, first_sum, second_sum):
        both = jnp.concatenate([jnp.sum(first_sum, axis=0, keepdims=True), jnp.sum(second_sum, axis=0, keepdims=True)], axis=1)
        parts = jnp.dot(limbs(both), group[...], preferred_element_type=F32)
        stat_all[par, h, me] = parts[0:1] + parts[1:2] + parts[2:3]
        for peer in peers:
            pltpu.make_async_remote_copy(src_ref=stat_all.at[par, h, me], dst_ref=stat_all.at[par, h, me], send_sem=ssend.at[par, h],
                                         recv_sem=srecv.at[par, h], device_id=peer, device_id_type=MESH).start()

    def stats_wait(par, h):
        several = stat_all.at[par, h, pl.ds(0, n_dev - 1)]
        pltpu.make_async_copy(several, several, srecv.at[par, h]).wait()
        pltpu.make_async_copy(several, several, ssend.at[par, h]).wait()

    def vector(ref, i, h):
        return ref[i // 2, pl.ds(i % 2, 1), h * half:(h + 1) * half]

    chan = lax.broadcasted_iota(jnp.int32, (2 * half, LANES), 0)
    lane = lax.broadcasted_iota(jnp.int32, (2 * half, LANES), 1)
    first = jnp.where(lane < LANES // 2, lane * per_group, (lane - LANES // 2) * per_group + half)
    limit = jnp.where(lane < LANES // 2, half, 2 * half)
    member = (chan >= first) & (chan < first + per_group) & (first < limit)
    group[...] = jnp.where(member, 1.0, 0.0).astype(BF16)
    wyb[...] = jnp.zeros_like(wyb)
    xt[...] = jnp.zeros_like(xt)
    zt[...] = jnp.zeros_like(zt)

    def tile_sums(values):
        total = values[0:SLOTS]
        for c in range(1, n_col):
            total = total + values[c * SLOTS:(c + 1) * SLOTS]
        return total

    def no_sums(width):
        return jnp.zeros((SLOTS, width), F32), jnp.zeros((SLOTS, width), F32)

    def load_row(r, carry):
        for f in range(n_frame):
            moved = x_ref[f, r].astype(F32)
            for k in range(n_chan // LANES):
                xt[k, pl.ds(f, n_col, stride=SLOTS), :] = moved[:, k * LANES:(k + 1) * LANES]
        values = jnp.concatenate([xt[k] for k in range(n_chan // LANES)], axis=1)
        hidden[r] = values.astype(BF16)
        for h in range(2):
            part = values[:, h * half:(h + 1) * half]
            ex[0, h, r + 1] = part.astype(BF16)
            cols[0, h, 0, r] = part[0:SLOTS].astype(BF16)
            cols[0, h, 1, r] = part[main - SLOTS:main].astype(BF16)
        for c in range(n_col):
            zt[c * SLOTS:c * SLOTS + n_frame, 0:z_ref.shape[3]] = z_ref[r, c].astype(F32)
        latent = zt[...]
        zx[r + 1] = latent.astype(BF16)
        zcols[0, r] = latent[0:SLOTS].astype(BF16)
        zcols[1, r] = latent[main - SLOTS:main].astype(BF16)
        return carry[0] + tile_sums(values), carry[1] + tile_sums(values * values)

    start_sums = lax.fori_loop(0, n_row, load_row, no_sums(n_chan))

    pl.semaphore_wait(barrier, n_dev - 1)
    z_copies = halo_copies(zx, zcolx, zcols, zsend, zrecv)
    for h in range(2):
        stats_send(0, h, start_sums[0][:, h * half:(h + 1) * half], start_sums[1][:, h * half:(h + 1) * half])
        if h == 0:
            for copy in z_copies:
                copy.start()
        for copy in block_halo(0, h):
            copy.start()
    for copy in z_copies:
        copy.wait()

    @pl.loop(0, n_row + 2)
    def _(r):
        zext[r] = jnp.concatenate([zcolx[0, r].astype(F32), zx[r].astype(F32), zcolx[1, r].astype(F32)], axis=0).astype(BF16)

    row_of = lax.broadcasted_iota(jnp.int32, (wide, half), 0)
    slot_of = lax.broadcasted_iota(jnp.int32, (n_col + 2, SLOTS, half), 1)
    first_valid = jnp.where(sw == 0, SLOTS, 0)
    last_valid = jnp.where(sw == n_sw - 1, wide - SLOTS, wide)

    def inside(r):
        beyond = ((r == 0) & (sh == 0)) | ((r == n_row + 1) & (sh == n_sh - 1))
        end = jnp.where(beyond, 0, last_valid)
        return (row_of >= first_valid) & (row_of < end)

    def wide_row(par, h, r):
        return jnp.concatenate([colx[par, h, 0, r].astype(F32), ex[par, h, r].astype(F32), colx[par, h, 1, r].astype(F32)], axis=0)

    frame_of = lax.broadcasted_iota(jnp.int32, (n_col, SLOTS, half), 1).reshape(main, half)

    def activate(i, par, h):
        stats_wait(par, h)
        total = stat_all[par, h, 0]
        for d in range(1, n_dev):
            total = total + stat_all[par, h, d]
        total = total / count
        group_var = jnp.maximum(pltpu.roll(total, LANES // 2, 1) - total * total, 0.0)
        parts = contract_lanes(limbs(jnp.concatenate([total, lax.rsqrt(group_var + GN_EPSILON)], axis=0)), group[0:half])
        chan_both = parts[0:2] + parts[2:4] + parts[4:6]
        mean = chan_both[0:1]
        scale = chan_both[1:2] * vector(gain_ref, i, h)
        shift = vector(shift_ref, i, h)
        for copy in block_halo(par, h):
            copy.wait()

        @pl.loop(0, n_row + 2)
        def _(r):
            normed = (wide_row(par, h, r) - mean) * scale + shift
            mixed = normed * yb[r, :, h * half:(h + 1) * half] + yb[r, :, n_chan + h * half:n_chan + (h + 1) * half]
            act = jnp.where(inside(r), mixed * jax.nn.sigmoid(mixed), 0.0)
            taps = act.reshape(n_col + 2, SLOTS, half)
            for kt in (2, 1, 0):
                for dw in range(3):
                    xk[h, kt, r, :, dw * half:(dw + 1) * half] = taps[dw:dw + n_col].reshape(main, half).astype(BF16)
                if kt > 0:
                    taps = jnp.where(slot_of == 0, taps, pltpu.roll(taps, 1, 1))

    def taps_of(h):
        return jnp.concatenate([xk[h, kt, dh:dh + n_row].reshape(n_row * main, 3 * half) for kt in range(3) for dh in range(3)], axis=1)

    def release(g):
        @pl.loop(g, g + 3)
        def _(k):
            weight_start(k + RING)

    def conv_step(i, _):
        par = i % 2
        after = (i + 1) % 2
        g = 6 * i

        wyb[0:zyw_ref.shape[1], 0:n_chan] = zyw_ref[i]
        wyb[0:zyw_ref.shape[1], n_chan:2 * n_chan] = zbw_ref[i]
        maps = jnp.dot(zext[...].reshape((n_row + 2) * wide, LANES), wyb[...], preferred_element_type=F32)
        map_bias = jnp.concatenate([vector(ref, i, h) for ref in (zyb_ref, zbb_ref) for h in range(2)], axis=1)
        yb[...] = (maps + map_bias).reshape(n_row + 2, wide, 2 * n_chan)

        activate(i, par, 0)
        for kt in range(3):
            weight_wait(g + kt)
        acc[...] = contract_lanes(taps_of(0), jnp.concatenate([wbuf[(g + kt) % RING] for kt in range(3)], axis=1))
        release(g)
        activate(i, par, 1)
        for kt in range(3):
            weight_wait(g + 3 + kt)

        second = i % 2 == 1

        def out_half(o, _):
            chans = pl.ds(pl.multiple_of(o * half, half), half)
            w = jnp.concatenate([wbuf[(g + 3 + kt) % RING, chans, :] for kt in range(3)], axis=1)
            acc[:, chans] = acc[:, chans] + contract_lanes(taps_of(1), w)
            bias = cb_ref[i // 2, pl.ds(i % 2, 1), chans]

            def finish_row(r, carry):
                conv = (acc[pl.ds(pl.multiple_of(r * main, main), main), chans] + bias).astype(BF16).astype(F32)
                old = hidden[r, :, chans].astype(F32)
                value = jnp.where(second, old + conv, conv).astype(BF16).astype(F32)
                value = jnp.where(frame_of < n_frame, value, 0.0)
                hidden[r, :, chans] = jnp.where(second, value, old).astype(BF16)
                ex[after, o, r + 1] = value.astype(BF16)
                cols[after, o, 0, r] = value[0:SLOTS].astype(BF16)
                cols[after, o, 1, r] = value[main - SLOTS:main].astype(BF16)
                return carry[0] + tile_sums(value), carry[1] + tile_sums(value * value)

            sums = lax.fori_loop(0, n_row, finish_row, no_sums(half))

            @pl.when(i < n_conv - 1)
            def _():
                stats_send(after, o, *sums)

            for copy in block_halo(after, o):
                copy.start()
            return 0

        lax.fori_loop(0, 2, out_half, 0)
        release(g + 3)
        return 0

    lax.fori_loop(0, n_conv, conv_step, 0)

    par = n_conv % 2

    def edges(h):
        for copy in block_halo(par, h):
            copy.wait()

        @pl.loop(0, n_row + 2)
        def _(r):
            value = jnp.where(inside(r), wide_row(par, h, r), 0.0).astype(BF16)
            xk[h, 0, r, :, 0:half] = value[0:main]
            xk[h, 1, r, 0:2 * SLOTS, 0:half] = value[main:wide]

    def products(h, dy):
        begin = jnp.minimum(dy, 1)
        rows = pl.ds(begin, n_row + 1)
        lhs = jnp.concatenate([xk[h, 0, rows, :, 0:half], xk[h, 1, rows, 0:2 * SLOTS, 0:half]], axis=1)
        lhs = lhs.reshape((n_row + 1) * wide, half)
        for dx in range(3):
            w = wbuf[(last_group + h) % RING, :, pl.ds(pl.multiple_of((dy * 3 + dx) * half, half), half)]
            product = contract_lanes(lhs, w).reshape(n_row + 1, wide, n_chan)
            lanes = slice(dx * n_chan, (dx + 1) * n_chan)
            prod[dy, :, :, lanes] = product if h == 0 else prod[dy, :, :, lanes] + product

    for h in range(2):
        edges(h)
        weight_wait(last_group + h)

        @pl.loop(0, 3)
        def _(dy):
            products(h, dy)

    up_bias = ub_ref[...]

    @pl.loop(0, n_row)
    def _(r):
        for py in range(2):
            def of(dx, lo):
                at = (slice(lo, lo + main), slice(dx * n_chan, (dx + 1) * n_chan))
                return prod[(0, r + py) + at] + prod[(1, r) + at] + prod[(2, r + py) + at]

            middle = of(1, SLOTS) + up_bias
            phases = [of(0, 0) + middle + of(2, SLOTS), of(0, SLOTS) + middle + of(2, 2 * SLOTS)]
            tiles = [phases[px][c * SLOTS:(c + 1) * SLOTS] for c in range(n_col) for px in range(2)]
            y_ref[2 * r + py] = jnp.concatenate(tiles, axis=0).astype(BF16)


def solution(mesh):
    n_sh = mesh.shape["sh"]
    n_sw = mesh.shape["sw"]

    def local_step(features, latent, gn_gain, gn_bias, zy_weight, zy_bias, zb_weight, zb_bias, conv_weight, conv_bias, up_weight, up_bias):
        _, n_chan, n_frame, n_row, n_col = features.shape
        n_latent = latent.shape[1]
        n_conv = gn_gain.shape[0] * gn_gain.shape[1]
        main = n_col * SLOTS
        wide = main + 2 * SLOTS
        n_dev = n_sh * n_sw
        half = n_chan // 2

        small = lambda values: values.reshape(n_conv, n_latent, n_chan)
        taps = jnp.transpose(conv_weight, (0, 1, 4, 5, 6, 2, 3)).reshape(3 * n_conv, 9, n_chan, n_chan)
        up_taps = jnp.transpose(up_weight, (2, 3, 0, 1)).reshape(9, n_chan, n_chan)
        dims = (n_sh, n_sw, n_frame, n_row, n_col, n_chan, n_conv)
        vmem = pl.BlockSpec(memory_space=pltpu.VMEM)
        hbm = pl.BlockSpec(memory_space=pl.ANY)
        dma = pltpu.SemaphoreType.DMA
        rows = n_row + 2
        result = pl.pallas_call(
            functools.partial(block_kernel, dims),
            out_shape=jax.ShapeDtypeStruct((2 * n_row, 2 * main, n_chan), BF16),
            in_specs=[vmem] * 8 + [hbm, vmem, hbm, vmem],
            out_specs=vmem,
            scratch_shapes=[
                pltpu.VMEM((2, 2, rows, main, half), BF16),
                pltpu.VMEM((2, 2, 2, rows, SLOTS, half), BF16),
                pltpu.VMEM((2, 2, 2, n_row, SLOTS, half), BF16),
                pltpu.VMEM((rows, main, LANES), BF16),
                pltpu.VMEM((2, rows, SLOTS, LANES), BF16),
                pltpu.VMEM((2, n_row, SLOTS, LANES), BF16),
                pltpu.VMEM((rows, wide, LANES), BF16),
                pltpu.VMEM((2, 2, n_dev, 1, LANES), F32),
                pltpu.VMEM((n_chan, LANES), BF16),
                pltpu.VMEM((LANES, 2 * n_chan), BF16),
                pltpu.VMEM((rows, wide, 2 * n_chan), F32),
                pltpu.VMEM((2, 3, rows, main, 3 * half), BF16),
                pltpu.VMEM((n_row * main, n_chan), F32),
                pltpu.VMEM((n_row, main, n_chan), BF16),
                pltpu.VMEM((RING, n_chan, 9 * half), BF16),
                pltpu.VMEM((3, n_row + 1, wide, 3 * n_chan), F32),
                pltpu.VMEM((n_chan // LANES, main, LANES), F32),
                pltpu.VMEM((main, LANES), F32),
                dma((RING,)),
                dma((2, 2, 8)),
                dma((2, 2, 8)),
                dma((8,)),
                dma((8,)),
                dma((2, 2)),
                dma((2, 2)),
            ],
            compiler_params=pltpu.CompilerParams(collective_id=0, has_side_effects=True, vmem_limit_bytes=64 * 1024 * 1024 - 65536 - 4096),
            name="decoder_block",
        )(jnp.transpose(features[0], (1, 2, 3, 0)), jnp.transpose(latent[0], (2, 3, 1, 0)), gn_gain, gn_bias, small(zy_weight), zy_bias,
          small(zb_weight), zb_bias, taps, conv_bias, up_taps, up_bias.reshape(1, n_chan))
        frames = result.reshape(2 * n_row, 2 * n_col, SLOTS, n_chan)[:, :, :n_frame]
        return jnp.transpose(frames, (3, 2, 0, 1))[None]

    data_spec = P("dp", None, None, "sh", "sw")
    return jax.shard_map(local_step, mesh=mesh, in_specs=(data_spec, data_spec) + (P(),) * 10, out_specs=data_spec, check_vma=False)
```

time: 108 us -> 85.2 us (0.79)
  Pallas kernels: 93.4 us -> 79.3 us
  local copies, waits for them, and re-layouts: 14.6 us -> 5.81 us
    pallas_call x1, Pallas kernels: 93.4 us -> 79.3 us  [local_step(): pl.pallas_call(functools.partial(block_kernel, dims), out_shape=jax.Shape...]
    reshape x7 -> x0, local copies, waits for them, and re-layouts: 8.17 us -> none  [the longest x5 6.53 us: local_step(): vector = lambda values: values.reshape(n_conv, 1, n_chan)]
    unnamed x3 -> x2, local copies, waits for them, and re-layouts: 6.45 us -> 5.81 us
where the time goes in v2:
time: 85.2 us; the launch traced here: 85.1 us
  Pallas kernels  79.3 us (93%)
  local copies, waits for them, and re-layouts  5.81 us (7%)
    pallas_call x1, Pallas kernels, local_step(): pl.pallas_call(functools.partial(block_kernel, dims), out_shape=jax.Shape...  79.3 us
    unnamed x2, local copies, waits for them, and re-layouts  5.81 us

profile of v2, /device:TPU:97, one launch (start us, length us, event | category | flops | bytes accessed | tf_op | source)
XLA Modules:
  0.0 85.1 jit_solution(16139483687066308294)
XLA Ops:
  0.0 2.0 %copy.13 = bf16[1,16,6,12,6]{1,2,4,3,0:T(8,128)(2,1)} copy(bf16[1,16,6,12,6]{3,1,4,2,0:T(8,128)(2,1)} %param.13) | data formatting | bytes 27648 | tf_op args[1]
  2.0 79.3 %decoder_block.1 = bf16[24,96,512]{2,1,0:T(8,128)(2,1)} custom-call(bf16[6,12,6,512]{3,2,1,0:T(8,128)(2,1)} %bitcast.25, bf16[12,6,6,16]{3,2,1,0:T(8,128)(2,1)} %bitcast.26, f32[2,2,512]{2,1,0:T(2,128)} %gain_ref.1, f32[2,2,512]{2,1,0:T(2,128)} %shift_ref.1, bf16[4,16,512]{2,1,0:T(8,128)(2,1)} %bitcast.27, f32[2,2,512]{2,1,0:T(2,128)} %zyb_ref.1, ...), custom_call_target="tpu_custom_call" | custom-call | tf_op jit(solution)/shard_map/decoder_block/pallas_call | solution.py:344
  81.2 3.8 %copy.17 = bf16[24,12,6,512]{3,0,1,2:T(8,128)(2,1)} copy(bf16[24,12,6,512]{3,2,1,0:T(8,128)(2,1)} %bitcast.23) | data formatting | bytes 3538944

commit v3 on v2

--- a/solution.py
+++ b/solution.py
@@ -47,37 +47,33 @@
     up, down = (sh + n_sh - 1) % n_sh, (sh + 1) % n_sh
     left, right = (sw + n_sw - 1) % n_sw, (sw + 1) % n_sw
 
+    barrier = pltpu.get_barrier_semaphore()
+    hops = lambda a, b: min(a, n_sw - a) + min(b, n_sh - b) / 2
+    offsets = sorted(((a, b) for a in range(n_sw) for b in range(n_sh)), key=lambda ab: -hops(*ab))[:-1]
+    rows_of, cols_of = [(sh + b) % n_sh for b in range(n_sh)], [(sw + a) % n_sw for a in range(n_sw)]
+    peers = [{"sh": rows_of[b], "sw": cols_of[a]} for a, b in offsets]
+    for peer in peers:
+        pl.semaphore_signal(barrier, inc=1, device_id=peer, device_id_type=MESH)
+
     last_group = 6 * n_conv
 
-    def weight_start(g):
-        slot = g % RING
-        source = (g // 6) * 3 + g % 3
-        from_half = (g // 3) % 2
-        for tap in range(9):
-            dst = wbuf.at[slot, :, pl.ds(tap * half, half)]
-
-            @pl.when(g < last_group)
-            def _():
-                lanes = pl.ds(pl.multiple_of(from_half * half, half), half)
-                pltpu.make_async_copy(cw_ref.at[jnp.minimum(source, 3 * n_conv - 1), tap, :, lanes], dst, wsem.at[slot]).start()
-
-            @pl.when((g >= last_group) & (g < last_group + 2))
-            def _():
-                lanes = pl.ds(pl.multiple_of(jnp.clip(g - last_group, 0, 1) * half, half), half)
-                pltpu.make_async_copy(uw_ref.at[tap, :, lanes], dst, wsem.at[slot]).start()
+    def conv_weights(i, h):
+        for kt in range(3):
+            slot = (6 * i + 3 * h + kt) % RING
+            pltpu.make_async_copy(cw_ref.at[3 * i + kt, :, :, pl.ds(h * half, half)], wbuf.at[slot], wsem.at[slot]).start()
+
+    def up_weights():
+        for h in range(2):
+            slot = (last_group + h) % RING
+            pltpu.make_async_copy(uw_ref.at[:, :, pl.ds(h * half, half)], wbuf.at[slot], wsem.at[slot]).start()
 
     def weight_wait(g):
         slot = g % RING
         pltpu.make_async_copy(wbuf.at[slot], wbuf.at[slot], wsem.at[slot]).wait()
 
-    @pl.loop(0, RING)
-    def _(g):
-        weight_start(g)
-
-    barrier = pltpu.get_barrier_semaphore()
-    peers = [{"sh": (sh + b) % n_sh, "sw": (sw + a) % n_sw} for a in range(n_sw) for b in range(n_sh)][1:]
-    for peer in peers:
-        pl.semaphore_signal(barrier, inc=1, device_id=peer, device_id_type=MESH)
+    conv_weights(0, 0)
+    conv_weights(0, 1)
+    conv_weights(1, 0)
 
     def halo_copies(rows, recv_cols, send_cols, send_sem, recv_sem):
         table = [
@@ -96,10 +92,13 @@
     def block_halo(par, h):
         return halo_copies(ex.at[par, h], colx.at[par, h], cols.at[par, h], hsend.at[par, h], hrecv.at[par, h])
 
-    def stats_send(par, h, first_sum, second_sum):
+    def group_row(h, first_sum, second_sum):
         both = jnp.concatenate([jnp.sum(first_sum, axis=0, keepdims=True), jnp.sum(second_sum, axis=0, keepdims=True)], axis=1)
-        parts = jnp.dot(limbs(both), group[...], preferred_element_type=F32)
-        stat_all[par, h, me] = parts[0:1] + parts[1:2] + parts[2:3]
+        parts = jnp.dot(limbs(both), group[h], preferred_element_type=F32)
+        return parts[0:1] + parts[1:2] + parts[2:3]
+
+    def stats_send(par, h, row):
+        stat_all[par, h, me] = row
         for peer in peers:
             pltpu.make_async_remote_copy(src_ref=stat_all.at[par, h, me], dst_ref=stat_all.at[par, h, me], send_sem=ssend.at[par, h],
                                          recv_sem=srecv.at[par, h], device_id=peer, device_id_type=MESH).start()
@@ -114,10 +113,12 @@
 
     chan = lax.broadcasted_iota(jnp.int32, (2 * half, LANES), 0)
     lane = lax.broadcasted_iota(jnp.int32, (2 * half, LANES), 1)
-    first = jnp.where(lane < LANES // 2, lane * per_group, (lane - LANES // 2) * per_group + half)
-    limit = jnp.where(lane < LANES // 2, half, 2 * half)
-    member = (chan >= first) & (chan < first + per_group) & (first < limit)
-    group[...] = jnp.where(member, 1.0, 0.0).astype(BF16)
+    squares = lane >= LANES // 2
+    for h in range(2):
+        first = jnp.where(squares, lane - LANES // 2, lane) * per_group - h * half
+        held = (first >= 0) & (first < half)
+        first = first + jnp.where(squares, half, 0)
+        group[h] = jnp.where(held & (chan >= first) & (chan < first + per_group), 1.0, 0.0).astype(BF16)
     wyb[...] = jnp.zeros_like(wyb)
     xt[...] = jnp.zeros_like(xt)
     zt[...] = jnp.zeros_like(zt)
@@ -155,13 +156,13 @@
 
     pl.semaphore_wait(barrier, n_dev - 1)
     z_copies = halo_copies(zx, zcolx, zcols, zsend, zrecv)
-    for h in range(2):
-        stats_send(0, h, start_sums[0][:, h * half:(h + 1) * half], start_sums[1][:, h * half:(h + 1) * half])
-        if h == 0:
-            for copy in z_copies:
-                copy.start()
-        for copy in block_halo(0, h):
-            copy.start()
+    stats_send(0, 0, sum(group_row(h, start_sums[0][:, h * half:(h + 1) * half], start_sums[1][:, h * half:(h + 1) * half]) for h in range(2)))
+    for copy in block_halo(0, 0):
+        copy.start()
+    for copy in z_copies:
+        copy.start()
+    for copy in block_halo(0, 1):
+        copy.start()
     for copy in z_copies:
         copy.wait()
 
@@ -185,13 +186,22 @@
     frame_of = lax.broadcasted_iota(jnp.int32, (n_col, SLOTS, half), 1).reshape(main, half)
 
     def activate(i, par, h):
-        stats_wait(par, h)
-        total = stat_all[par, h, 0]
+        if h == 0:
+            row = 0
+            stats_wait(par, 0)
+        else:
+            row = jnp.minimum(i, 1)
+
+            @pl.when(i > 0)
+            def _():
+                stats_wait(par, 1)
+
+        total = stat_all[par, row, 0]
         for d in range(1, n_dev):
-            total = total + stat_all[par, h, d]
+            total = total + stat_all[par, row, d]
         total = total / count
         group_var = jnp.maximum(pltpu.roll(total, LANES // 2, 1) - total * total, 0.0)
-        parts = contract_lanes(limbs(jnp.concatenate([total, lax.rsqrt(group_var + GN_EPSILON)], axis=0)), group[0:half])
+        parts = contract_lanes(limbs(jnp.concatenate([total, lax.rsqrt(group_var + GN_EPSILON)], axis=0)), group[h, 0:half])
         chan_both = parts[0:2] + parts[2:4] + parts[4:6]
         mean = chan_both[0:1]
         scale = chan_both[1:2] * vector(gain_ref, i, h)
@@ -214,10 +224,8 @@
     def taps_of(h):
         return jnp.concatenate([xk[h, kt, dh:dh + n_row].reshape(n_row * main, 3 * half) for kt in range(3) for dh in range(3)], axis=1)
 
-    def release(g):
-        @pl.loop(g, g + 3)
-        def _(k):
-            weight_start(k + RING)
+    def weights_of(g, chans):
+        return jnp.concatenate([wbuf[(g + kt) % RING, tap, chans] for kt in range(3) for tap in range(9)], axis=1)
 
     def conv_step(i, _):
         par = i % 2
@@ -233,8 +241,12 @@
         activate(i, par, 0)
         for kt in range(3):
             weight_wait(g + kt)
-        acc[...] = contract_lanes(taps_of(0), jnp.concatenate([wbuf[(g + kt) % RING] for kt in range(3)], axis=1))
-        release(g)
+        acc[...] = contract_lanes(taps_of(0), weights_of(g, slice(None)))
+
+        @pl.when(i < n_conv - 1)
+        def _():
+            conv_weights(i + 1, 1)
+
         activate(i, par, 1)
         for kt in range(3):
             weight_wait(g + 3 + kt)
@@ -243,8 +255,7 @@
 
         def out_half(o, _):
             chans = pl.ds(pl.multiple_of(o * half, half), half)
-            w = jnp.concatenate([wbuf[(g + 3 + kt) % RING, chans, :] for kt in range(3)], axis=1)
-            acc[:, chans] = acc[:, chans] + contract_lanes(taps_of(1), w)
+            acc[:, chans] = acc[:, chans] + contract_lanes(taps_of(1), weights_of(g + 3, chans))
             bias = cb_ref[i // 2, pl.ds(i % 2, 1), chans]
 
             def finish_row(r, carry):
@@ -259,17 +270,28 @@
                 return carry[0] + tile_sums(value), carry[1] + tile_sums(value * value)
 
             sums = lax.fori_loop(0, n_row, finish_row, no_sums(half))
+            copies = block_halo(after, o)
+            for copy in copies[0:2]:
+                copy.start()
 
             @pl.when(i < n_conv - 1)
             def _():
-                stats_send(after, o, *sums)
-
-            for copy in block_halo(after, o):
+                stats_send(after, o, group_row(o, *sums))
+
+            for copy in copies[2:]:
                 copy.start()
             return 0
 
         lax.fori_loop(0, 2, out_half, 0)
-        release(g + 3)
+
+        @pl.when(i < n_conv - 2)
+        def _():
+            conv_weights(i + 2, 0)
+
+        @pl.when(i == n_conv - 2)
+        def _():
+            up_weights()
+
         return 0
 
     lax.fori_loop(0, n_conv, conv_step, 0)
@@ -292,7 +314,7 @@
         lhs = jnp.concatenate([xk[h, 0, rows, :, 0:half], xk[h, 1, rows, 0:2 * SLOTS, 0:half]], axis=1)
         lhs = lhs.reshape((n_row + 1) * wide, half)
         for dx in range(3):
-            w = wbuf[(last_group + h) % RING, :, pl.ds(pl.multiple_of((dy * 3 + dx) * half, half), half)]
+            w = wbuf[(last_group + h) % RING, dy * 3 + dx]
             product = contract_lanes(lhs, w).reshape(n_row + 1, wide, n_chan)
             lanes = slice(dx * n_chan, (dx + 1) * n_chan)
             prod[dy, :, :, lanes] = product if h == 0 else prod[dy, :, :, lanes] + product
@@ -355,13 +377,13 @@
                 pltpu.VMEM((2, n_row, SLOTS, LANES), BF16),
                 pltpu.VMEM((rows, wide, LANES), BF16),
                 pltpu.VMEM((2, 2, n_dev, 1, LANES), F32),
-                pltpu.VMEM((n_chan, LANES), BF16),
+                pltpu.VMEM((2, n_chan, LANES), BF16),
                 pltpu.VMEM((LANES, 2 * n_chan), BF16),
                 pltpu.VMEM((rows, wide, 2 * n_chan), F32),
                 pltpu.VMEM((2, 3, rows, main, 3 * half), BF16),
                 pltpu.VMEM((n_row * main, n_chan), F32),
                 pltpu.VMEM((n_row, main, n_chan), BF16),
-                pltpu.VMEM((RING, n_chan, 9 * half), BF16),
+                pltpu.VMEM((RING, 9, n_chan, half), BF16),
                 pltpu.VMEM((3, n_row + 1, wide, 3 * n_chan), F32),
                 pltpu.VMEM((n_chan // LANES, main, LANES), F32),
                 pltpu.VMEM((main, LANES), F32),

time: 85.2 us -> 84.1 us (0.987)
  Pallas kernels: 79.3 us -> 78.2 us
    pallas_call x1, Pallas kernels: 79.3 us -> 78.2 us  [local_step(): pl.pallas_call(functools.partial(block_kernel, dims), out_shape=jax.Shape...]
where the time goes in v3:
time: 84.1 us; the launch traced here: 84 us
  Pallas kernels  78.2 us (93%)
  local copies, waits for them, and re-layouts  5.81 us (7%)
    pallas_call x1, Pallas kernels, local_step(): pl.pallas_call(functools.partial(block_kernel, dims), out_shape=jax.Shape...  78.2 us
    unnamed x2, local copies, waits for them, and re-layouts  5.81 us

profile of v3, /device:TPU:97, one launch (start us, length us, event | category | flops | bytes accessed | tf_op | source)
XLA Modules:
  0.0 84.0 jit_solution(17260788017830800369)
XLA Ops:
  0.0 2.0 %copy.13 = bf16[1,16,6,12,6]{1,2,4,3,0:T(8,128)(2,1)} copy(bf16[1,16,6,12,6]{3,1,4,2,0:T(8,128)(2,1)} %param.13) | data formatting | bytes 27648 | tf_op args[1]
  2.0 78.2 %decoder_block.1 = bf16[24,96,512]{2,1,0:T(8,128)(2,1)} custom-call(bf16[6,12,6,512]{3,2,1,0:T(8,128)(2,1)} %bitcast.25, bf16[12,6,6,16]{3,2,1,0:T(8,128)(2,1)} %bitcast.26, f32[2,2,512]{2,1,0:T(2,128)} %gain_ref.1, f32[2,2,512]{2,1,0:T(2,128)} %shift_ref.1, bf16[4,16,512]{2,1,0:T(8,128)(2,1)} %bitcast.27, f32[2,2,512]{2,1,0:T(2,128)} %zyb_ref.1, ...), custom_call_target="tpu_custom_call" | custom-call | tf_op jit(solution)/shard_map/decoder_block/pallas_call | solution.py:366
  80.1 3.8 %copy.17 = bf16[24,12,6,512]{3,0,1,2:T(8,128)(2,1)} copy(bf16[24,12,6,512]{3,2,1,0:T(8,128)(2,1)} %bitcast.23) | data formatting | bytes 3538944

commit v4 on v3

--- a/solution.py
+++ b/solution.py
@@ -32,7 +32,7 @@
 
 
 def block_kernel(dims, x_ref, z_ref, gain_ref, shift_ref, zyw_ref, zyb_ref, zbw_ref, zbb_ref, cw_ref, cb_ref, uw_ref, ub_ref, y_ref,
-                 ex, colx, cols, zx, zcolx, zcols, zext, stat_all, group, wyb, yb, xk, acc, hidden, wbuf, prod, xt, zt,
+                 ex, colx, cols, zx, zcolx, zcols, zext, stat_all, group, wyb, yb, xk, acc, hidden, wbuf, prod, xt, zs, zt, ybuf,
                  wsem, hsend, hrecv, zsend, zrecv, ssend, srecv):
     n_sh, n_sw, n_frame, n_row, n_col, n_chan, n_conv = dims
     half = n_chan // 2
@@ -121,7 +121,22 @@
         group[h] = jnp.where(held & (chan >= first) & (chan < first + per_group), 1.0, 0.0).astype(BF16)
     wyb[...] = jnp.zeros_like(wyb)
     xt[...] = jnp.zeros_like(xt)
+    zs[...] = jnp.zeros_like(zs)
     zt[...] = jnp.zeros_like(zt)
+
+    n_latent = z_ref.shape[2]
+    for f in range(n_frame):
+        for c in range(n_col):
+            k = (f * n_col + c) * n_latent
+            zs[k:k + n_latent, 0:n_row] = z_ref[f, c].astype(F32)
+    turned = zs[...].T
+    for f in range(n_frame):
+        for c in range(n_col):
+            block, lane_at = divmod((f * n_col + c) * n_latent, LANES)
+            moved = turned[0:2 * SLOTS, block * LANES:(block + 1) * LANES]
+            if lane_at:
+                moved = pltpu.roll(moved, LANES - lane_at, 1)
+            zt[pl.ds(c * SLOTS + f, n_row, stride=main), :] = moved[0:n_row]
 
     def tile_sums(values):
         total = values[0:SLOTS]
@@ -144,9 +159,7 @@
             ex[0, h, r + 1] = part.astype(BF16)
             cols[0, h, 0, r] = part[0:SLOTS].astype(BF16)
             cols[0, h, 1, r] = part[main - SLOTS:main].astype(BF16)
-        for c in range(n_col):
-            zt[c * SLOTS:c * SLOTS + n_frame, 0:z_ref.shape[3]] = z_ref[r, c].astype(F32)
-        latent = zt[...]
+        latent = zt[pl.ds(pl.multiple_of(r * main, main), main), :]
         zx[r + 1] = latent.astype(BF16)
         zcols[0, r] = latent[0:SLOTS].astype(BF16)
         zcols[1, r] = latent[main - SLOTS:main].astype(BF16)
@@ -232,8 +245,8 @@
         after = (i + 1) % 2
         g = 6 * i
 
-        wyb[0:zyw_ref.shape[1], 0:n_chan] = zyw_ref[i]
-        wyb[0:zyw_ref.shape[1], n_chan:2 * n_chan] = zbw_ref[i]
+        wyb[0:n_latent, 0:n_chan] = zyw_ref[i]
+        wyb[0:n_latent, n_chan:2 * n_chan] = zbw_ref[i]
         maps = jnp.dot(zext[...].reshape((n_row + 2) * wide, LANES), wyb[...], preferred_element_type=F32)
         map_bias = jnp.concatenate([vector(ref, i, h) for ref in (zyb_ref, zbb_ref) for h in range(2)], axis=1)
         yb[...] = (maps + map_bias).reshape(n_row + 2, wide, 2 * n_chan)
@@ -338,8 +351,18 @@
 
             middle = of(1, SLOTS) + up_bias
             phases = [of(0, 0) + middle + of(2, SLOTS), of(0, SLOTS) + middle + of(2, 2 * SLOTS)]
-            tiles = [phases[px][c * SLOTS:(c + 1) * SLOTS] for c in range(n_col) for px in range(2)]
-            y_ref[2 * r + py] = jnp.concatenate(tiles, axis=0).astype(BF16)
+            for c in range(n_col):
+                for px in range(2):
+                    tile = phases[px][c * SLOTS:(c + 1) * SLOTS]
+                    for k in range(n_chan // LANES):
+                        rows = pl.ds((2 * c + px) * SLOTS * 2 * n_row + 2 * r + py, SLOTS, stride=2 * n_row)
+                        ybuf[k, rows, :] = tile[:, k * LANES:(k + 1) * LANES]
+
+    @pl.loop(0, 2 * n_col)
+    def _(c):
+        for f in range(n_frame):
+            rows = pl.ds(pl.multiple_of((c * SLOTS + f) * 2 * n_row, SLOTS), 2 * n_row)
+            y_ref[f, c] = jnp.concatenate([ybuf[k, rows, :] for k in range(n_chan // LANES)], axis=1).astype(BF16)
 
 
 def solution(mesh):
@@ -365,7 +388,7 @@
         rows = n_row + 2
         result = pl.pallas_call(
             functools.partial(block_kernel, dims),
-            out_shape=jax.ShapeDtypeStruct((2 * n_row, 2 * main, n_chan), BF16),
+            out_shape=jax.ShapeDtypeStruct((n_frame, 2 * n_col, 2 * n_row, n_chan), BF16),
             in_specs=[vmem] * 8 + [hbm, vmem, hbm, vmem],
             out_specs=vmem,
             scratch_shapes=[
@@ -386,7 +409,9 @@
                 pltpu.VMEM((RING, 9, n_chan, half), BF16),
                 pltpu.VMEM((3, n_row + 1, wide, 3 * n_chan), F32),
                 pltpu.VMEM((n_chan // LANES, main, LANES), F32),
-                pltpu.VMEM((main, LANES), F32),
+                pltpu.VMEM((pl.cdiv(n_frame * n_col * n_latent, LANES) * LANES, LANES), F32),
+                pltpu.VMEM((n_row * main, LANES), F32),
+                pltpu.VMEM((n_chan // LANES, 2 * n_col * SLOTS * 2 * n_row, LANES), F32),
                 dma((RING,)),
                 dma((2, 2, 8)),
                 dma((2, 2, 8)),
@@ -397,10 +422,9 @@
             ],
             compiler_params=pltpu.CompilerParams(collective_id=0, has_side_effects=True, vmem_limit_bytes=64 * 1024 * 1024 - 65536 - 4096),
             name="decoder_block",
-        )(jnp.transpose(features[0], (1, 2, 3, 0)), jnp.transpose(latent[0], (2, 3, 1, 0)), gn_gain, gn_bias, small(zy_weight), zy_bias,
+        )(jnp.transpose(features[0], (1, 2, 3, 0)), jnp.transpose(latent[0], (1, 3, 0, 2)), gn_gain, gn_bias, small(zy_weight), zy_bias,
           small(zb_weight), zb_bias, taps, conv_bias, up_taps, up_bias.reshape(1, n_chan))
-        frames = result.reshape(2 * n_row, 2 * n_col, SLOTS, n_chan)[:, :, :n_frame]
-        return jnp.transpose(frames, (3, 2, 0, 1))[None]
+        return jnp.transpose(result, (3, 0, 2, 1))[None]
 
     data_spec = P("dp", None, None, "sh", "sw")
     return jax.shard_map(local_step, mesh=mesh, in_specs=(data_spec, data_spec) + (P(),) * 10, out_specs=data_spec, check_vma=False)

time: 84.1 us -> 81.9 us (0.974)
  local copies, waits for them, and re-layouts: 5.81 us -> 2.88 us
    unnamed x2 -> x1, local copies, waits for them, and re-layouts: 5.81 us -> 2.88 us
where the time goes in v4:
time: 81.9 us; the launch traced here: 81.8 us
  Pallas kernels  78.9 us (96%)
  local copies, waits for them, and re-layouts  2.88 us (4%)
    pallas_call x1, Pallas kernels, local_step(): pl.pallas_call(functools.partial(block_kernel, dims), out_shape=jax.Shape...  78.9 us
    unnamed x1, local copies, waits for them, and re-layouts  2.88 us

profile of v4, /device:TPU:97, one launch (start us, length us, event | category | flops | bytes accessed | tf_op | source)
XLA Modules:
  0.0 81.8 jit_solution(14539612318054192864)
XLA Ops:
  0.0 78.9 %decoder_block.1 = bf16[6,12,24,512]{3,2,1,0:T(8,128)(2,1)} custom-call(bf16[6,12,6,512]{3,2,1,0:T(8,128)(2,1)} %bitcast.21, bf16[6,6,16,12]{3,2,1,0:T(8,128)(2,1)} %bitcast.22, f32[2,2,512]{2,1,0:T(2,128)} %gain_ref.1, f32[2,2,512]{2,1,0:T(2,128)} %shift_ref.1, bf16[4,16,512]{2,1,0:T(8,128)(2,1)} %bitcast.23, f32[2,2,512]{2,1,0:T(2,128)} %zyb_ref.1, ...), custom_call_target="tpu_custom_call" | custom-call | tf_op jit(solution)/shard_map/decoder_block/pallas_call | solution.py:389
  78.9 2.9 %copy.14 = bf16[1,512,6,24,12]{1,3,4,2,0:T(8,128)(2,1)} copy(bf16[1,512,6,24,12]{1,3,4,2,0:T(8,128)(2,1)} %bitcast.19) | data formatting | bytes 3538944

commit v5 on v4

--- a/solution.py
+++ b/solution.py
@@ -268,11 +268,12 @@
 
         def out_half(o, _):
             chans = pl.ds(pl.multiple_of(o * half, half), half)
-            acc[:, chans] = acc[:, chans] + contract_lanes(taps_of(1), weights_of(g + 3, chans))
+            part = contract_lanes(taps_of(1), weights_of(g + 3, chans))
             bias = cb_ref[i // 2, pl.ds(i % 2, 1), chans]
 
             def finish_row(r, carry):
-                conv = (acc[pl.ds(pl.multiple_of(r * main, main), main), chans] + bias).astype(BF16).astype(F32)
+                at = slice(r * main, (r + 1) * main)
+                conv = (acc[at, chans] + part[at] + bias).astype(BF16).astype(F32)
                 old = hidden[r, :, chans].astype(F32)
                 value = jnp.where(second, old + conv, conv).astype(BF16).astype(F32)
                 value = jnp.where(frame_of < n_frame, value, 0.0)
@@ -282,7 +283,9 @@
                 cols[after, o, 1, r] = value[main - SLOTS:main].astype(BF16)
                 return carry[0] + tile_sums(value), carry[1] + tile_sums(value * value)
 
-            sums = lax.fori_loop(0, n_row, finish_row, no_sums(half))
+            sums = no_sums(half)
+            for r in range(n_row):
+                sums = finish_row(r, sums)
             copies = block_halo(after, o)
             for copy in copies[0:2]:
                 copy.start()

time: 81.9 us -> 80.9 us (0.988)
  Pallas kernels: 78.9 us -> 77.9 us
    pallas_call x1, Pallas kernels: 78.9 us -> 77.9 us  [local_step(): pl.pallas_call(functools.partial(block_kernel, dims), out_shape=jax.Shape...]
where the time goes in v5:
time: 80.9 us; the launch traced here: 80.8 us
  Pallas kernels  77.9 us (96%)
  local copies, waits for them, and re-layouts  2.88 us (4%)
    pallas_call x1, Pallas kernels, local_step(): pl.pallas_call(functools.partial(block_kernel, dims), out_shape=jax.Shape...  77.9 us
    unnamed x1, local copies, waits for them, and re-layouts  2.88 us

profile of v5, /device:TPU:97, one launch (start us, length us, event | category | flops | bytes accessed | tf_op | source)
XLA Modules:
  0.0 80.8 jit_solution(1320466075350996631)
XLA Ops:
  0.0 77.9 %decoder_block.1 = bf16[6,12,24,512]{3,2,1,0:T(8,128)(2,1)} custom-call(bf16[6,12,6,512]{3,2,1,0:T(8,128)(2,1)} %bitcast.21, bf16[6,6,16,12]{3,2,1,0:T(8,128)(2,1)} %bitcast.22, f32[2,2,512]{2,1,0:T(2,128)} %gain_ref.1, f32[2,2,512]{2,1,0:T(2,128)} %shift_ref.1, bf16[4,16,512]{2,1,0:T(8,128)(2,1)} %bitcast.23, f32[2,2,512]{2,1,0:T(2,128)} %zyb_ref.1, ...), custom_call_target="tpu_custom_call" | custom-call | tf_op jit(solution)/shard_map/decoder_block/pallas_call | solution.py:392
  77.9 2.9 %copy.14 = bf16[1,512,6,24,12]{1,3,4,2,0:T(8,128)(2,1)} copy(bf16[1,512,6,24,12]{1,3,4,2,0:T(8,128)(2,1)} %bitcast.19) | data formatting | bytes 3538944
